TPU v7x, 128 devices: a whole 4x4x4 slice. The times are simulated.
128 devices in a mesh: seq: 8 (over y, core), span: 16 (over x, z).
Axes of the slice: x: 4, y: 4, z: 4, core: 2. Of those that a mesh axis runs over, the one named last changes fastest.
Arguments:
- queries: bfloat16 [16, 1024, 1536], P('span', 'seq'), may hold values from -6 to 6
- key_head_matrix: bfloat16 [16, 1024, 512], P('span', 'seq'), may hold values from -6 to 6
- value_head_matrix: bfloat16 [16, 1024, 512], P('span', 'seq'), may hold values from -6 to 6
- attn_output: bfloat16 [16, 1024, 1536], P('span', 'seq'), may hold values from -6 to 6
- out_grad: bfloat16 [16, 1024, 1536], P('span', 'seq'), may hold values from -6 to 6
Outputs:
- query_grad: bfloat16 [16, 1024, 1536], P('span', 'seq')
- key_grad: bfloat16 [16, 1024, 512], P('span', 'seq')
- value_grad: bfloat16 [16, 1024, 512], P('span', 'seq')
All inputs are finite; a program needn't handle non-finite values.
Results may differ from a plain program's by a relative error of at most 0.005.
Values may be sent and summed in bfloat16 or wider, within the bound.
A program may use at most 64 MiB of HBM per device.

v0:
```python
import math

import jax
import jax.numpy as jnp
from jax import lax
from jax.sharding import PartitionSpec as P

HEAD_WIDTH = 64
QUERY_PER_KEY = 3


NEG_LARGE = -1e30


def sent_together(arrays, axis, dim, along):
    ends, at = ([], 0)
    for a in arrays[:-1]:
        at += a.shape[along]
        ends.append(at)
    both = jnp.concatenate(arrays, axis=along)
    return tuple(
        jnp.split(lax.psum_scatter(both, axis, scatter_dimension=dim, tiled=True), ends, axis=along)
    )


def spread_rows(source, seq_count):
    return source.reshape(source.shape[1], seq_count, source.shape[2] // seq_count)


def over_blocks(update, running, arrays, offset, block_rows, live_test):
    row_total = arrays[0].shape[0]
    block_total = row_total // block_rows

    def visit(block_number, running_state):
        first_row = block_number * block_rows
        slices = tuple(
            (lax.dynamic_slice_in_dim(member, first_row, block_rows, 0) for member in arrays)
        )
        position = offset + first_row
        return lax.cond(
            live_test(position),
            lambda current: update(current, slices, position),
            lambda current: current,
            running_state,
        )

    return lax.fori_loop(0, block_total, visit, running)


def per_device(queries, key_head_matrix, value_head_matrix, attn_output, out_grad):
    seq_count = lax.axis_size("seq")
    own_block = lax.axis_index("span")
    tok_local = queries.shape[1]
    kv_local = key_head_matrix.shape[2] // (HEAD_WIDTH * seq_count)
    block_len = tok_local * seq_count
    scaling = 1.0 / math.sqrt(HEAD_WIDTH)
    exchanged = (
        lax.all_to_all(
            spread_rows(queries, seq_count), "seq", split_axis=1, concat_axis=0, tiled=True
        ),
        lax.all_to_all(
            spread_rows(out_grad, seq_count), "seq", split_axis=1, concat_axis=0, tiled=True
        ),
        lax.all_to_all(
            spread_rows(attn_output, seq_count), "seq", split_axis=1, concat_axis=0, tiled=True
        ),
        lax.all_to_all(
            spread_rows(key_head_matrix, seq_count), "seq", split_axis=1, concat_axis=0, tiled=True
        ),
        lax.all_to_all(
            spread_rows(value_head_matrix, seq_count),
            "seq",
            split_axis=1,
            concat_axis=0,
            tiled=True,
        ),
    )
    query_flat = exchanged[0].reshape(block_len, kv_local * QUERY_PER_KEY * HEAD_WIDTH)
    grad_flat = exchanged[1].reshape(block_len, kv_local * QUERY_PER_KEY * HEAD_WIDTH)
    query_split = query_flat.reshape(block_len, kv_local, QUERY_PER_KEY, HEAD_WIDTH)
    grad_split = grad_flat.reshape(block_len, kv_local, QUERY_PER_KEY, HEAD_WIDTH)
    output_split = exchanged[2].reshape(block_len, kv_local, QUERY_PER_KEY, HEAD_WIDTH)
    key_flat = exchanged[3].reshape(block_len, kv_local * HEAD_WIDTH)
    value_flat = exchanged[4].reshape(block_len, kv_local * HEAD_WIDTH)
    row_delta = jnp.transpose(
        jnp.sum(grad_split.astype(jnp.float32) * output_split.astype(jnp.float32), axis=3),
        (1, 2, 0),
    )
    own_first = own_block * block_len
    query_pos = own_first + lax.iota(jnp.int32, block_len)

    def key_live(position):
        return position < own_first + block_len

    def key_scores(key_block, position):
        rows_here = key_block.shape[0]
        key_split = key_block.reshape(rows_here, kv_local, HEAD_WIDTH)
        scores = (
            jnp.einsum("tgjd,rgd->gjtr", query_split, key_split, preferred_element_type=jnp.float32)
            * scaling
        )
        key_pos = position + lax.iota(jnp.int32, rows_here)
        allowed = key_pos[None, :] <= query_pos[:, None]
        return (key_split, scores, allowed)

    def stats_update(running_state, slices, position):
        row_max, row_sum = running_state
        key_split, scores, allowed = key_scores(slices[0], position)
        masked = jnp.where(allowed, scores, NEG_LARGE)
        new_max = jnp.maximum(row_max, jnp.max(masked, axis=3))
        weights = jnp.where(allowed, jnp.exp(scores - new_max[..., None]), 0.0)
        new_sum = row_sum * jnp.exp(row_max - new_max) + jnp.sum(weights, axis=3)
        return (new_max, new_sum)

    stats_init = (
        jnp.full((kv_local, QUERY_PER_KEY, block_len), NEG_LARGE, jnp.float32),
        jnp.zeros((kv_local, QUERY_PER_KEY, block_len), jnp.float32),
    )
    key_whole, value_whole = (
        lax.all_gather(key_flat, "span", axis=0, tiled=True),
        lax.all_gather(value_flat, "span", axis=0, tiled=True),
    )
    row_max, row_sum = over_blocks(stats_update, stats_init, (key_whole,), 0, block_len, key_live)
    log_norm = row_max + jnp.log(row_sum)

    def key_side(slices, position):
        key_split, scores, allowed = key_scores(slices[0], position)
        value_split = slices[1].reshape(slices[1].shape[0], kv_local, HEAD_WIDTH)
        prob_weights = jnp.where(allowed, jnp.exp(scores - log_norm[..., None]), 0.0)
        prob_grad = jnp.einsum(
            "tgjd,rgd->gjtr", grad_split, value_split, preferred_element_type=jnp.float32
        )
        score_low = (prob_weights * (prob_grad - row_delta[..., None])).astype(jnp.bfloat16)
        query_term = scaling * jnp.einsum(
            "gjtr,rgd->tgjd", score_low, key_split, preferred_element_type=jnp.float32
        )
        return (prob_weights, score_low, query_term)

    def partial_update(running_state, slices, position):
        query_acc, key_acc, value_acc = running_state
        prob_weights, score_low, query_term = key_side(slices, position)
        rows_here = slices[0].shape[0]
        key_term = scaling * jnp.einsum(
            "gjtr,tgjd->rgd", score_low, query_split, preferred_element_type=jnp.float32
        )
        value_term = jnp.einsum(
            "gjtr,tgjd->rgd",
            prob_weights.astype(jnp.bfloat16),
            grad_split,
            preferred_element_type=jnp.float32,
        )
        key_acc = lax.dynamic_update_slice_in_dim(
            key_acc, key_term.reshape(rows_here, kv_local * HEAD_WIDTH), position, 0
        )
        value_acc = lax.dynamic_update_slice_in_dim(
            value_acc, value_term.reshape(rows_here, kv_local * HEAD_WIDTH), position, 0
        )
        return (query_acc + query_term, key_acc, value_acc)

    query_zero = jnp.zeros((block_len, kv_local, QUERY_PER_KEY, HEAD_WIDTH), jnp.float32)
    buffer_zero = jnp.zeros((lax.axis_size("span") * block_len, kv_local * HEAD_WIDTH), jnp.float32)
    grad_init = (query_zero, buffer_zero, buffer_zero)
    grad_result = over_blocks(
        partial_update, grad_init, (key_whole, value_whole), 0, block_len, key_live
    )
    query_acc, key_acc, value_acc = grad_result
    key_total, value_total = sent_together((key_acc, value_acc), "span", 0, 1)
    query_out = query_acc.astype(jnp.bfloat16).reshape(
        seq_count, tok_local, kv_local * QUERY_PER_KEY * HEAD_WIDTH
    )
    key_result = key_total.astype(jnp.bfloat16).reshape(seq_count, tok_local, kv_local * HEAD_WIDTH)
    value_result = value_total.astype(jnp.bfloat16).reshape(
        seq_count, tok_local, kv_local * HEAD_WIDTH
    )
    returned = (
        lax.all_to_all(query_out, "seq", split_axis=0, concat_axis=2, tiled=True),
        lax.all_to_all(key_result, "seq", split_axis=0, concat_axis=2, tiled=True),
        lax.all_to_all(value_result, "seq", split_axis=0, concat_axis=2, tiled=True),
    )
    return (returned[0], returned[1], returned[2])


def solution(mesh):
    in_specs = (
        P("span", "seq", None),
        P("span", "seq", None),
        P("span", "seq", None),
        P("span", "seq", None),
        P("span", "seq", None),
    )
    out_specs = (P("span", "seq", None), P("span", "seq", None), P("span", "seq", None))
    return jax.shard_map(
        per_device, mesh=mesh, in_specs=in_specs, out_specs=out_specs, check_vma=False
    )
```

profile of v0, /device:TPU:99, one launch (start us, length us, event | category | flops | bytes accessed | tf_op | source)
XLA Modules:
  0.0 666.5 jit_solution(363014363874218583)
XLA Ops:
  8.2 10.2 %all_to_all.123 = bf16[128,8,64]{0,2,1:T(8,128)(2,1)S(1)} all-to-all(bf16[128,8,64]{0,2,1:T(8,128)(2,1)S(1)} %bitcast.200), channel_id=1, replica_groups=mesh['seq'=8,'span'=16] {'seq'}, dimensions={1} | all-to-all | bytes 262144 | tf_op jit(solution)/shard_map/all_to_all | solution.py:67
  20.3 8.5 %all_to_all.124 = bf16[128,8,64]{0,2,1:T(8,128)(2,1)S(1)} all-to-all(bf16[128,8,64]{0,2,1:T(8,128)(2,1)S(1)} %bitcast.201), channel_id=1, replica_groups=mesh['seq'=8,'span'=16] {'seq'}, dimensions={1} | all-to-all | bytes 262144 | tf_op jit(solution)/shard_map/all_to_all | solution.py:70
  31.5 4.2 all-to-all-start.1
  37.6 5.8 all-to-all-done.1
  43.4 4.6 all-to-all-start.4
  49.9 5.9 all-to-all-done.4
  55.8 4.5 all-to-all-start.3
  61.3 6.8 %all-to-all-done.3 = bf16[128,8,192]{0,2,1:T(8,128)(2,1)S(1)} async-done(((bf16[128,8,192]{0,2,1:T(8,128)(2,1)}), bf16[128,8,192]{0,2,1:T(8,128)(2,1)S(1)}, u32[]{:S(2)}, u32[]{:S(2)}) %all-to-all-start.3) | async-done | bytes 393248 | tf_op jit(solution)/shard_map/all_to_all | solution.py:61
  69.2 66.9 %while.38 = (s32[]{:T(128)}, f32[1,3,1024]{2,1,0:T(4,128)S(1)}, f32[1,3,1024]{2,1,0:T(4,128)S(1)}, s32[]{:T(128)}, bf16[16384,64]{0,1:T(8,128)(2,1)}, /*index=5*...) while((s32[]{:T(128)}, f32[1,3,1024]{2,1,0:T(4,128)S(1)}, ...), condition=%wide.region_5.6_spmd.clone, body=%wide.region_0.5_spmd.clone.sunk | while | flops 425730048 | bytes 33214752 | solution.py:47
  69.2 8.2 %conditional.6 = ((f32[1,3,1024]{2,1,0:T(4,128)S(1)}, f32[1,3,1024]{2,1,0:T(4,128)S(1)})) conditional(s32[]{:T(128)} %convert_element_type.97, (f32[1,3,1024]{2,1,0:T(4,128)S(1)}, f32[1,3,1024]{2,1,0:T(4,128)S(1)}) %tuple.120, (s32[]{:T(128)}, s32[]{:T(128)}, bf16[16384,64]{0,1:T(8,128)(2,1)}, bf16[1024,1,3,64]{0,3,2,1:T(8,128)(2,1)S(1)}, ...), branch_computations={%region_1.1_spmd, %region_2.4_spmd} | conditional | flops 425730048 | bytes 33210466 | solution.py:40
  77.5 8.3 %conditional.6 = ((f32[1,3,1024]{2,1,0:T(4,128)S(1)}, f32[1,3,1024]{2,1,0:T(4,128)S(1)})) conditional(s32[]{:T(128)} %convert_element_type.97, (f32[1,3,1024]{2,1,0:T(4,128)S(1)}, f32[1,3,1024]{2,1,0:T(4,128)S(1)}) %tuple.120, (s32[]{:T(128)}, s32[]{:T(128)}, bf16[16384,64]{0,1:T(8,128)(2,1)}, bf16[1024,1,3,64]{0,3,2,1:T(8,128)(2,1)S(1)}, ...), branch_computations={%region_1.1_spmd, %region_2.4_spmd} | conditional | flops 425730048 | bytes 33210466 | solution.py:40
  85.8 8.3 %conditional.6 = ((f32[1,3,1024]{2,1,0:T(4,128)S(1)}, f32[1,3,1024]{2,1,0:T(4,128)S(1)})) conditional(s32[]{:T(128)} %convert_element_type.97, (f32[1,3,1024]{2,1,0:T(4,128)S(1)}, f32[1,3,1024]{2,1,0:T(4,128)S(1)}) %tuple.120, (s32[]{:T(128)}, s32[]{:T(128)}, bf16[16384,64]{0,1:T(8,128)(2,1)}, bf16[1024,1,3,64]{0,3,2,1:T(8,128)(2,1)S(1)}, ...), branch_computations={%region_1.1_spmd, %region_2.4_spmd} | conditional | flops 425730048 | bytes 33210466 | solution.py:40
  94.1 8.3 %conditional.6 = ((f32[1,3,1024]{2,1,0:T(4,128)S(1)}, f32[1,3,1024]{2,1,0:T(4,128)S(1)})) conditional(s32[]{:T(128)} %convert_element_type.97, (f32[1,3,1024]{2,1,0:T(4,128)S(1)}, f32[1,3,1024]{2,1,0:T(4,128)S(1)}) %tuple.120, (s32[]{:T(128)}, s32[]{:T(128)}, bf16[16384,64]{0,1:T(8,128)(2,1)}, bf16[1024,1,3,64]{0,3,2,1:T(8,128)(2,1)S(1)}, ...), branch_computations={%region_1.1_spmd, %region_2.4_spmd} | conditional | flops 425730048 | bytes 33210466 | solution.py:40
  102.4 8.3 %conditional.6 = ((f32[1,3,1024]{2,1,0:T(4,128)S(1)}, f32[1,3,1024]{2,1,0:T(4,128)S(1)})) conditional(s32[]{:T(128)} %convert_element_type.97, (f32[1,3,1024]{2,1,0:T(4,128)S(1)}, f32[1,3,1024]{2,1,0:T(4,128)S(1)}) %tuple.120, (s32[]{:T(128)}, s32[]{:T(128)}, bf16[16384,64]{0,1:T(8,128)(2,1)}, bf16[1024,1,3,64]{0,3,2,1:T(8,128)(2,1)S(1)}, ...), branch_computations={%region_1.1_spmd, %region_2.4_spmd} | conditional | flops 425730048 | bytes 33210466 | solution.py:40
  110.8 8.3 %conditional.6 = ((f32[1,3,1024]{2,1,0:T(4,128)S(1)}, f32[1,3,1024]{2,1,0:T(4,128)S(1)})) conditional(s32[]{:T(128)} %convert_element_type.97, (f32[1,3,1024]{2,1,0:T(4,128)S(1)}, f32[1,3,1024]{2,1,0:T(4,128)S(1)}) %tuple.120, (s32[]{:T(128)}, s32[]{:T(128)}, bf16[16384,64]{0,1:T(8,128)(2,1)}, bf16[1024,1,3,64]{0,3,2,1:T(8,128)(2,1)S(1)}, ...), branch_computations={%region_1.1_spmd, %region_2.4_spmd} | conditional | flops 425730048 | bytes 33210466 | solution.py:40
  119.1 8.3 %conditional.6 = ((f32[1,3,1024]{2,1,0:T(4,128)S(1)}, f32[1,3,1024]{2,1,0:T(4,128)S(1)})) conditional(s32[]{:T(128)} %convert_element_type.97, (f32[1,3,1024]{2,1,0:T(4,128)S(1)}, f32[1,3,1024]{2,1,0:T(4,128)S(1)}) %tuple.120, (s32[]{:T(128)}, s32[]{:T(128)}, bf16[16384,64]{0,1:T(8,128)(2,1)}, bf16[1024,1,3,64]{0,3,2,1:T(8,128)(2,1)S(1)}, ...), branch_computations={%region_1.1_spmd, %region_2.4_spmd} | conditional | flops 425730048 | bytes 33210466 | solution.py:40
  127.4 8.3 %conditional.6 = ((f32[1,3,1024]{2,1,0:T(4,128)S(1)}, f32[1,3,1024]{2,1,0:T(4,128)S(1)})) conditional(s32[]{:T(128)} %convert_element_type.97, (f32[1,3,1024]{2,1,0:T(4,128)S(1)}, f32[1,3,1024]{2,1,0:T(4,128)S(1)}) %tuple.120, (s32[]{:T(128)}, s32[]{:T(128)}, bf16[16384,64]{0,1:T(8,128)(2,1)}, bf16[1024,1,3,64]{0,3,2,1:T(8,128)(2,1)S(1)}, ...), branch_computations={%region_1.1_spmd, %region_2.4_spmd} | conditional | flops 425730048 | bytes 33210466 | solution.py:40
  141.7 169.6 %while.39 = (s32[]{:T(128)}, f32[1024,1,3,64]{0,3,2,1:T(8,128)}, f32[16384,64]{0,1:T(8,128)}, f32[16384,64]{0,1:T(8,128)}, s32[]{:T(128)}, /*index=5*/bf16[16384...) while((s32[]{:T(128)}, f32[1024,1,3,64]{0,3,2,1:T(8,128)}, ...), condition=%wide.region_10.11_spmd.clone, body=%wide.region_7.10_spmd.clone.sunk | while | flops 2046232576 | bytes 63893872 | solution.py:47
  141.7 21.1 %conditional.7 = ((f32[1024,1,3,64]{0,3,2,1:T(8,128)}, f32[16384,64]{0,1:T(8,128)}, f32[16384,64]{0,1:T(8,128)})) conditional(s32[]{:T(128)} %convert_element_type.98, (f32[1024,1,3,64]{0,3,2,1:T(8,128)}, f32[16384,64]{0,1:T(8,128)}, f32[16384,64]{0,1:T(8,128)}) %tuple.123, (s32[]{:T(128)}, bf16[16384,64]{0,1:T(8,128)(2,1)}, s32[]{:T(128)}, ...), branch_computations={%region_8.8_spmd, %region_9.9_spmd} | conditional | flops 2046232576 | bytes 63889500 | solution.py:40
  146.1 5.9 fusion.19
  152.0 4.9 fusion.30
  162.9 21.2 %conditional.7 = ((f32[1024,1,3,64]{0,3,2,1:T(8,128)}, f32[16384,64]{0,1:T(8,128)}, f32[16384,64]{0,1:T(8,128)})) conditional(s32[]{:T(128)} %convert_element_type.98, (f32[1024,1,3,64]{0,3,2,1:T(8,128)}, f32[16384,64]{0,1:T(8,128)}, f32[16384,64]{0,1:T(8,128)}) %tuple.123, (s32[]{:T(128)}, bf16[16384,64]{0,1:T(8,128)(2,1)}, s32[]{:T(128)}, ...), branch_computations={%region_8.8_spmd, %region_9.9_spmd} | conditional | flops 2046232576 | bytes 63889500 | solution.py:40
  167.2 5.9 fusion.19
  173.1 4.9 fusion.30
  184.0 21.2 %conditional.7 = ((f32[1024,1,3,64]{0,3,2,1:T(8,128)}, f32[16384,64]{0,1:T(8,128)}, f32[16384,64]{0,1:T(8,128)})) conditional(s32[]{:T(128)} %convert_element_type.98, (f32[1024,1,3,64]{0,3,2,1:T(8,128)}, f32[16384,64]{0,1:T(8,128)}, f32[16384,64]{0,1:T(8,128)}) %tuple.123, (s32[]{:T(128)}, bf16[16384,64]{0,1:T(8,128)(2,1)}, s32[]{:T(128)}, ...), branch_computations={%region_8.8_spmd, %region_9.9_spmd} | conditional | flops 2046232576 | bytes 63889500 | solution.py:40
  188.4 5.9 fusion.19
  194.3 4.9 fusion.30
  205.2 21.2 %conditional.7 = ((f32[1024,1,3,64]{0,3,2,1:T(8,128)}, f32[16384,64]{0,1:T(8,128)}, f32[16384,64]{0,1:T(8,128)})) conditional(s32[]{:T(128)} %convert_element_type.98, (f32[1024,1,3,64]{0,3,2,1:T(8,128)}, f32[16384,64]{0,1:T(8,128)}, f32[16384,64]{0,1:T(8,128)}) %tuple.123, (s32[]{:T(128)}, bf16[16384,64]{0,1:T(8,128)(2,1)}, s32[]{:T(128)}, ...), branch_computations={%region_8.8_spmd, %region_9.9_spmd} | conditional | flops 2046232576 | bytes 63889500 | solution.py:40
  209.6 5.8 fusion.19
  215.5 4.9 fusion.30
  226.4 21.1 %conditional.7 = ((f32[1024,1,3,64]{0,3,2,1:T(8,128)}, f32[16384,64]{0,1:T(8,128)}, f32[16384,64]{0,1:T(8,128)})) conditional(s32[]{:T(128)} %convert_element_type.98, (f32[1024,1,3,64]{0,3,2,1:T(8,128)}, f32[16384,64]{0,1:T(8,128)}, f32[16384,64]{0,1:T(8,128)}) %tuple.123, (s32[]{:T(128)}, bf16[16384,64]{0,1:T(8,128)(2,1)}, s32[]{:T(128)}, ...), branch_computations={%region_8.8_spmd, %region_9.9_spmd} | conditional | flops 2046232576 | bytes 63889500 | solution.py:40
  230.8 5.8 fusion.19
  236.6 4.9 fusion.30
  247.6 21.1 %conditional.7 = ((f32[1024,1,3,64]{0,3,2,1:T(8,128)}, f32[16384,64]{0,1:T(8,128)}, f32[16384,64]{0,1:T(8,128)})) conditional(s32[]{:T(128)} %convert_element_type.98, (f32[1024,1,3,64]{0,3,2,1:T(8,128)}, f32[16384,64]{0,1:T(8,128)}, f32[16384,64]{0,1:T(8,128)}) %tuple.123, (s32[]{:T(128)}, bf16[16384,64]{0,1:T(8,128)(2,1)}, s32[]{:T(128)}, ...), branch_computations={%region_8.8_spmd, %region_9.9_spmd} | conditional | flops 2046232576 | bytes 63889500 | solution.py:40
  251.9 5.8 fusion.19
  257.8 4.9 fusion.30
  268.7 21.2 %conditional.7 = ((f32[1024,1,3,64]{0,3,2,1:T(8,128)}, f32[16384,64]{0,1:T(8,128)}, f32[16384,64]{0,1:T(8,128)})) conditional(s32[]{:T(128)} %convert_element_type.98, (f32[1024,1,3,64]{0,3,2,1:T(8,128)}, f32[16384,64]{0,1:T(8,128)}, f32[16384,64]{0,1:T(8,128)}) %tuple.123, (s32[]{:T(128)}, bf16[16384,64]{0,1:T(8,128)(2,1)}, s32[]{:T(128)}, ...), branch_computations={%region_8.8_spmd, %region_9.9_spmd} | conditional | flops 2046232576 | bytes 63889500 | solution.py:40
  273.1 5.8 fusion.19
  279.0 4.9 fusion.30
  289.9 21.2 %conditional.7 = ((f32[1024,1,3,64]{0,3,2,1:T(8,128)}, f32[16384,64]{0,1:T(8,128)}, f32[16384,64]{0,1:T(8,128)})) conditional(s32[]{:T(128)} %convert_element_type.98, (f32[1024,1,3,64]{0,3,2,1:T(8,128)}, f32[16384,64]{0,1:T(8,128)}, f32[16384,64]{0,1:T(8,128)}) %tuple.123, (s32[]{:T(128)}, bf16[16384,64]{0,1:T(8,128)(2,1)}, s32[]{:T(128)}, ...), branch_computations={%region_8.8_spmd, %region_9.9_spmd} | conditional | flops 2046232576 | bytes 63889500 | solution.py:40
  294.2 5.9 fusion.19
  300.1 4.9 fusion.30
  311.4 7.5 %pad_maximum_fusion = f32[16384,128]{0,1:T(8,128)} fusion(f32[16384,64]{0,1:T(8,128)} %get-tuple-element.679, f32[16384,64]{0,1:T(8,128)} %get-tuple-element.678), kind=kLoop, calls=%fused_computation.56 | loop fusion | flops 2097152 | bytes 16777216 | tf_op jit(solution)/shard_map/concatenate | solution.py:20
  321.0 4.6 all-to-all-start.5
  325.6 310.8 %reduce-scatter.2.cloned.1.call-done = f32[1024,128]{0,1:T(8,128)} async-done(((f32[16384,128]{0,1:T(8,128)}), f32[1024,128]{0,1:T(8,128)}) %reduce-scatter.2.cloned.1.call-update) | async-done | bytes 524304 | tf_op jit(solution)/shard_map/reduce_scatter | solution.py:22
  638.2 6.4 all-to-all-start.7
  645.2 4.6 all-to-all-done.7
  649.8 4.1 all-to-all-start.6
  (204 shorter events, 176.9 us)
Async XLA Ops:
  7.2 61.6 %all-gather.3.cloned.1.call-start = ((), (), s32[]{:S(2)}) async-start(), calls=%async_computation.9 | async-start | bytes 2228224 | tf_op jit(solution)/shard_map/all_gather | solution.py:120
  19.2 116.9 %all-gather.5.cloned.1.call-start = ((), (), s32[]{:S(2)}) async-start(), calls=%async_computation.10 | async-start | bytes 2228224 | tf_op jit(solution)/shard_map/all_gather | solution.py:121
  31.5 11.9 %all-to-all-start.1 = ((bf16[128,8,192]{0,2,1:T(8,128)(2,1)}), bf16[128,8,192]{0,2,1:T(8,128)(2,1)S(1)}, u32[]{:S(2)}, u32[]{:S(2)}) async-start(bf16[128,8,192]{0,2,1:T(8,128)(2,1)} %bitcast.27), calls=%async_computation.1 | async-start | bytes 786432 | tf_op jit(solution)/shard_map/all_to_all | solution.py:58
  43.4 12.4 %all-to-all-start.4 = ((bf16[128,8,192]{0,2,1:T(8,128)(2,1)}), bf16[128,8,192]{0,2,1:T(8,128)(2,1)S(1)}, u32[]{:S(2)}, u32[]{:S(2)}) async-start(bf16[128,8,192]{0,2,1:T(8,128)(2,1)} %bitcast.36), calls=%async_computation.4 | async-start | bytes 786432 | tf_op jit(solution)/shard_map/all_to_all | solution.py:64
  55.8 12.2 %all-to-all-start.3 = ((bf16[128,8,192]{0,2,1:T(8,128)(2,1)}), bf16[128,8,192]{0,2,1:T(8,128)(2,1)S(1)}, u32[]{:S(2)}, u32[]{:S(2)}) async-start(bf16[128,8,192]{0,2,1:T(8,128)(2,1)} %bitcast.33), calls=%async_computation.3 | async-start | bytes 786432 | tf_op jit(solution)/shard_map/all_to_all | solution.py:61
  60.3 576.1 %reduce-scatter.2.cloned.1.call-start = ((), (), s32[]{:S(2)}) async-start(), calls=%async_computation.11 | async-start | bytes 8912896 | tf_op jit(solution)/shard_map/reduce_scatter | solution.py:22
  68.5 0.7 copy-start.1
  69.9 3.6 copy-start
  78.2 3.7 copy-start
  86.5 3.6 copy-start
  94.8 3.6 copy-start
  103.1 3.7 copy-start
  111.5 3.6 copy-start
  119.8 3.6 copy-start
  128.1 3.6 copy-start
  321.0 317.2 %all-to-all-start.5 = ((bf16[8,128,192]{1,2,0:T(8,128)(2,1)}), bf16[8,128,192]{1,2,0:T(8,128)(2,1)S(1)}, u32[]{:S(2)}, u32[]{:S(2)}) async-start(bf16[8,128,192]{1,2,0:T(8,128)(2,1)} %copy.64), calls=%async_computation.5 | async-start | bytes 786432 | tf_op jit(solution)/shard_map/all_to_all | solution.py:176
  638.2 11.6 %all-to-all-start.7 = ((bf16[8,128,64]{1,2,0:T(8,128)(2,1)}), bf16[8,128,64]{1,2,0:T(8,128)(2,1)S(1)}, u32[]{:S(2)}, u32[]{:S(2)}) async-start(bf16[8,128,64]{1,2,0:T(8,128)(2,1)} %bitcast.183), calls=%async_computation.8 | async-start | bytes 262144 | tf_op jit(solution)/shard_map/all_to_all | solution.py:178
  649.8 9.4 %all-to-all-start.6 = ((bf16[8,128,64]{1,2,0:T(8,128)(2,1)}), bf16[8,128,64]{1,2,0:T(8,128)(2,1)S(1)}, u32[]{:S(2)}, u32[]{:S(2)}) async-start(bf16[8,128,64]{1,2,0:T(8,128)(2,1)} %bitcast.184), calls=%async_computation.7 | async-start | bytes 262144 | tf_op jit(solution)/shard_map/all_to_all | solution.py:177
Sparse Core Ops, SparseCore 0:
  19.3 41.1 all-gather.2
  63.3 44.2 all-gather.4
  319.1 317.2 reduce-scatter.1
where the time goes:
time: 674 us; the launch traced here: 666 us
  waiting for transfers between devices  337 us (50%)
  matrix products  185 us (27%)
  other arithmetic  59.7 us (9%)
  starting transfers between devices  28.5 us (4%)
  local copies, waits for them, and re-layouts  21.5 us (3%)
  blocking collectives  18.7 us (3%)
  between operations  13.9 us (2%)
    reduce_scatter x1, waiting for transfers between devices, sent_together(): lax.psum_scatter(both, axis, scatter_dimension=dim, tiled=True)  311 us
    dot_general x16, matrix products, key_scores(): jnp.einsum('tgjd,rgd->gjtr', query_split, key_split, preferred_element_ty...  50.7 us
    dot_general x8, matrix products, key_side(): jnp.einsum('tgjd,rgd->gjtr', grad_split, value_split, preferred_element_t...  46.8 us
    dot_general x8, matrix products, partial_update(): jnp.einsum('gjtr,tgjd->rgd', prob_weights.astype(jnp.bfloat16), grad_spli...  39 us
    reduce_sum x8, other arithmetic, stats_update(): new_sum = row_sum * jnp.exp(row_max - new_max) + jnp.sum(weights, axis=3)  31 us
    dot_general x8, matrix products, key_side(): jnp.einsum('gjtr,rgd->tgjd', score_low, key_split, preferred_element_type...  26.7 us
    dot_general x8, matrix products, partial_update(): jnp.einsum('gjtr,tgjd->rgd', score_low, query_split, preferred_element_ty...  21.8 us
    le x16, other arithmetic, key_scores(): allowed = key_pos[None, :] <= query_pos[:, None]  18.3 us
  transfers between devices with their start and end apart: 9, of which 6 were waited for; matrix products, arithmetic and copies ran while one was open for 12% of the time, Pallas kernels for 0%

commit v1 on v0

v1 whole, which is shorter than its diff:
```python
import functools
import math

import jax
import jax.numpy as jnp
from jax import lax
from jax.experimental import pallas as pl
from jax.experimental.pallas import tpu as pltpu
from jax.sharding import PartitionSpec as P

HEAD_WIDTH = 64
QUERY_PER_KEY = 3
TILE = 512
CHUNK = 256
LANES = 128
NEG_LARGE = -1e30
SCORE_SCALE = 1.0 / math.sqrt(HEAD_WIDTH)
BASE2_SCALE = SCORE_SCALE * math.log2(math.e)
F32 = jnp.float32
BF16 = jnp.bfloat16


def dot(a, b, contract):
    return lax.dot_general(a, b, ((contract[0], contract[1]), ((), ())), preferred_element_type=F32)


def three_parts(x):
    first = x.astype(BF16).astype(F32)
    rest = x - first
    second = rest.astype(BF16).astype(F32)
    return first, second, rest - second


def compute_kernel(spans, qdo_ref, delta_ref, kv_ref, dq_ref, dkv_ref, lt, l2, ks1, ks2, vs1, stat_m, stat_l, dq_acc, p_buf, ds_buf):
    own = lax.axis_index("span")
    rows = QUERY_PER_KEY * TILE
    key_tiles = kv_ref.shape[0] // TILE
    diag = (2 * own, key_tiles - 1 - 2 * own)
    lane = lax.broadcasted_iota(jnp.int32, (TILE, LANES), 1)
    aux_s = jnp.where((lane >= 64) & (lane < 67), -1.0, 0.0)
    aux_v = jnp.where((lane >= 67) & (lane < 70), -1.0, 0.0).astype(BF16)

    @pl.loop(0, key_tiles)
    def _(t):
        at = pl.ds(pl.multiple_of(t * TILE, TILE), TILE)
        raw = kv_ref[at, :].astype(F32)
        scaled = raw * BASE2_SCALE
        high = scaled.astype(BF16).astype(F32)
        ks1[at, :] = jnp.where(lane < 64, high, 0.0).astype(BF16)
        ks2[at, :] = jnp.where(lane < 64, scaled - high, aux_s).astype(BF16)
        vs1[at, :] = jnp.where(lane >= 64, raw, 0.0).astype(BF16)
        dkv_ref[:, at] = jnp.zeros((LANES, TILE), F32)

    for u in range(2):
        for h in range(QUERY_PER_KEY):
            cols = pl.ds(h * TILE, TILE)
            turned = qdo_ref[u, h].astype(F32).T
            lt[u, 0:128, cols] = turned.astype(BF16)
            lt[u, 128:256, cols] = jnp.concatenate([turned[0:64], jnp.zeros((64, TILE), F32)], axis=0).astype(BF16)
        dq_acc[u] = jnp.zeros((rows, LANES), F32)
        stat_m[u] = jnp.full((8, rows), NEG_LARGE, F32)
        stat_l[u] = jnp.zeros((8, rows), F32)

    key_at = lax.broadcasted_iota(jnp.int32, (TILE, TILE), 0)
    query_at = lax.broadcasted_iota(jnp.int32, (TILE, TILE), 1)

    def stats(u, t, masked):
        at = pl.ds(pl.multiple_of(t * TILE, TILE), TILE)
        w = jnp.concatenate([ks1[at, :], ks2[at, :]], axis=1)
        for h in range(QUERY_PER_KEY):
            cols = pl.ds(h * TILE, TILE)
            s = dot(w, lt[u, :, cols], ((1,), (0,)))
            if masked:
                s = jnp.where(key_at <= query_at, s, NEG_LARGE)
            old = stat_m[u, 0:1, cols]
            new = jnp.maximum(old, jnp.max(s, axis=0, keepdims=True))
            e = jnp.exp2(s - new)
            part = jnp.sum(e.reshape(TILE // 8, 8, TILE), axis=0)
            stat_l[u, :, cols] = stat_l[u, :, cols] * jnp.exp2(old - new) + part
            stat_m[u, :, cols] = jnp.broadcast_to(new, (8, TILE))

    for u in range(2):
        @pl.loop(0, diag[u])
        def _(t):
            stats(u, t, False)

        stats(u, diag[u], True)

    row = lax.broadcasted_iota(jnp.int32, (16, TILE), 0)
    for u in range(2):
        for h in range(QUERY_PER_KEY):
            cols = pl.ds(h * TILE, TILE)
            total = jnp.sum(stat_l[u, :, cols], axis=0, keepdims=True)
            lse = stat_m[u, 0:1, cols] + jnp.log2(total)
            parts = three_parts(lse) + three_parts(delta_ref[u, h : h + 1, :])
            block = jnp.zeros((16, TILE), F32)
            for i, part in enumerate(parts):
                block = jnp.where(row == i, part, block)
            lt[u, 192:208, cols] = block.astype(BF16)
            l2[u, h] = lt[u, 128:256, cols].astype(F32).T.astype(BF16)

    def main(u, t, masked):
        at = pl.ds(pl.multiple_of(t * TILE, TILE), TILE)
        kw = jnp.concatenate([ks1[at, :], ks2[at, :]], axis=1)
        vw = jnp.concatenate([vs1[at, :], aux_v], axis=1)
        kv = kv_ref[at, :]
        if masked:
            key_col = lax.broadcasted_iota(jnp.int32, (CHUNK, TILE), 1)
            query_row = lax.broadcasted_iota(jnp.int32, (CHUNK, TILE), 0)
        for h in range(QUERY_PER_KEY):
            for first in range(0, TILE, CHUNK):
                here = pl.ds(h * TILE + first, CHUNK)
                lhs = jnp.concatenate([qdo_ref[u, h, first : first + CHUNK, :], l2[u, h, first : first + CHUNK, :]], axis=1)
                s = dot(lhs, kw, ((1,), (1,)))
                dp = dot(lhs, vw, ((1,), (1,)))
                p = jnp.exp2(s)
                if masked:
                    p = jnp.where(key_col <= query_row + first, p, 0.0)
                ds = (p * dp).astype(BF16)
                p_buf[here, :] = p.astype(BF16)
                ds_buf[here, :] = ds
                dq_acc[u, here, :] += dot(ds, kv, ((1,), (0,)))
        dkv_ref[0:64, at] += dot(lt[u, 0:64, :], ds_buf[...], ((1,), (0,)))
        dkv_ref[64:128, at] += dot(lt[u, 64:128, :], p_buf[...], ((1,), (0,)))

    for u in range(2):
        @pl.loop(0, diag[u])
        def _(t):
            main(u, t, False)

        main(u, diag[u], True)
        dq_ref[u] = (dq_acc[u] * SCORE_SCALE).astype(BF16)
    @pl.loop(0, key_tiles)
    def _(t):
        at = pl.ds(pl.multiple_of(t * TILE, TILE), TILE)
        dkv_ref[0:64, at] = dkv_ref[0:64, at] * SCORE_SCALE


def attention_grads(spans, qdo, delta, kv):
    rows = QUERY_PER_KEY * TILE
    keys = kv.shape[0]
    vmem = pl.BlockSpec(memory_space=pltpu.VMEM)
    return pl.pallas_call(
        functools.partial(compute_kernel, spans),
        out_shape=(
            jax.ShapeDtypeStruct((2, rows, LANES), BF16),
            jax.ShapeDtypeStruct((LANES, keys), F32),
        ),
        in_specs=[vmem] * 3,
        out_specs=(vmem, vmem),
        scratch_shapes=[
            pltpu.VMEM((2, 256, rows), BF16),
            pltpu.VMEM((2, QUERY_PER_KEY, TILE, LANES), BF16),
            pltpu.VMEM((keys, LANES), BF16),
            pltpu.VMEM((keys, LANES), BF16),
            pltpu.VMEM((keys, LANES), BF16),
            pltpu.VMEM((2, 8, rows), F32),
            pltpu.VMEM((2, 8, rows), F32),
            pltpu.VMEM((2, rows, LANES), F32),
            pltpu.VMEM((rows, TILE), BF16),
            pltpu.VMEM((rows, TILE), BF16),
        ],
        compiler_params=pltpu.CompilerParams(vmem_limit_bytes=60 * 1024 * 1024),
        name="attention_grads",
    )(qdo, delta, kv)


def per_device(queries, key_head_matrix, value_head_matrix, attn_output, out_grad):
    seqs = lax.axis_size("seq")
    spans = lax.axis_size("span")
    tokens = queries.shape[1]
    group = QUERY_PER_KEY * HEAD_WIDTH
    swap = [(i, spans - 1 - i) for i in range(spans)]

    q = queries.reshape(tokens, seqs, QUERY_PER_KEY, HEAD_WIDTH)
    do = out_grad.reshape(tokens, seqs, QUERY_PER_KEY, HEAD_WIDTH)
    o = attn_output.reshape(tokens, seqs, QUERY_PER_KEY, HEAD_WIDTH)
    qdo = jnp.transpose(jnp.concatenate([q, do], axis=3), (1, 2, 0, 3))
    delta = jnp.sum(do.astype(F32) * o.astype(F32), axis=3)
    delta = jnp.pad(jnp.transpose(delta, (1, 2, 0)), ((0, 0), (0, 5), (0, 0)))
    kv = jnp.concatenate(
        [
            key_head_matrix.reshape(tokens, seqs, HEAD_WIDTH),
            value_head_matrix.reshape(tokens, seqs, HEAD_WIDTH),
        ],
        axis=2,
    )
    kv = jnp.transpose(kv, (1, 0, 2))
    qdo = lax.all_to_all(qdo, "seq", split_axis=0, concat_axis=2, tiled=True)[0]
    delta = lax.all_to_all(delta, "seq", split_axis=0, concat_axis=2, tiled=True)[0]
    kv = lax.all_to_all(kv, "seq", split_axis=0, concat_axis=1, tiled=True)[0]
    kv = lax.all_gather(kv, "span", axis=0, tiled=True)
    qdo = jnp.stack([qdo[:, :TILE], lax.ppermute(qdo[:, TILE:], "span", swap)])
    delta = jnp.stack([delta[:, :TILE], lax.ppermute(delta[:, TILE:], "span", swap)])

    dq, dkv = attention_grads(spans, qdo, delta, kv)

    dkv = dkv.astype(BF16).reshape(LANES, spans, -1)
    dkv = lax.all_to_all(dkv, "span", split_axis=1, concat_axis=1, tiled=True)
    dkv = jnp.sum(dkv.astype(F32), axis=1).astype(BF16)
    dkv = jnp.transpose(dkv.reshape(LANES, seqs, tokens), (1, 2, 0))
    dkv = lax.all_to_all(dkv, "seq", split_axis=0, concat_axis=2, tiled=True)[0]
    dkv = dkv.reshape(tokens, seqs, 2, HEAD_WIDTH)
    dq = dq.reshape(2, QUERY_PER_KEY, TILE, LANES)[..., :HEAD_WIDTH]
    dq = jnp.transpose(dq, (0, 2, 1, 3)).reshape(2, TILE, group)
    dq = jnp.concatenate([dq[0], lax.ppermute(dq[1], "span", swap)], axis=0)
    dq = lax.all_to_all(dq.reshape(seqs, tokens, group), "seq", split_axis=0, concat_axis=2, tiled=True)
    return (
        dq,
        dkv[:, :, 0].reshape(1, tokens, seqs * HEAD_WIDTH),
        dkv[:, :, 1].reshape(1, tokens, seqs * HEAD_WIDTH),
    )


def solution(mesh):
    spec = P("span", "seq", None)
    return jax.shard_map(
        per_device, mesh=mesh, in_specs=(spec,) * 5, out_specs=(spec,) * 3, check_vma=False
    )
```

time: 674 us -> 309 us (0.46)
  waiting for transfers between devices: 337 us -> 100 us
  matrix products: 185 us -> 0 us
  Pallas kernels: 0 us -> 120 us
  other arithmetic: 59.7 us -> 10.5 us
  local copies, waits for them, and re-layouts: 21.5 us -> 12.3 us
    reduce_scatter x1 -> x0, waiting for transfers between devices: 311 us -> none  [sent_together(): lax.psum_scatter(both, axis, scatter_dimension=dim, tiled=True)]
    dot_general x48 -> x0, matrix products: 185 us -> none  [the longest x16 50.7 us: key_scores(): jnp.einsum('tgjd,rgd->gjtr', query_split, key_split, preferred_element_ty...]
    pallas_call x0 -> x1, Pallas kernels: none -> 120 us  [attention_grads(): pl.pallas_call(functools.partial(compute_kernel, spans), out_shape=(jax.S...]
    ppermute x0 -> x3, waiting for transfers between devices: none -> 59.5 us  [the longest x1 58.4 us: per_device(): dq = jnp.concatenate([dq[0], lax.ppermute(dq[1], 'span', swap)], axis=0)]
    reduce_sum x9 -> x2, other arithmetic: 31.2 us -> 3.28 us  [the longest x1 3.12 us: per_device(): dkv = jnp.sum(dkv.astype(F32), axis=1).astype(BF16)]
    all_gather x2 -> x1, waiting for transfers between devices: 0.04 us -> 19.6 us  [per_device(): kv = lax.all_gather(kv, 'span', axis=0, tiled=True)]
    le x16 -> x0, other arithmetic: 18.3 us -> none  [key_scores(): allowed = key_pos[None, :] <= query_pos[:, None]]
    concatenate x1 -> x0, other arithmetic: 7.53 us -> none  [sent_together(): both = jnp.concatenate(arrays, axis=along)]
  transfers between devices with their start and end apart: 9 -> 8, of which waited for: 6 -> 6; matrix products, arithmetic and copies ran while one was open for 12% -> 4% of each run, Pallas kernels for 0% -> 0%
where the time goes in v1:
time: 309 us; the launch traced here: 304 us
  Pallas kernels  120 us (39%)
  waiting for transfers between devices  100 us (32%)
  starting transfers between devices  26 us (8%)
  blocking collectives  19.9 us (6%)
  between operations  14.2 us (5%)
  local copies, waits for them, and re-layouts  12.3 us (4%)
  other arithmetic  10.5 us (3%)
    pallas_call x1, Pallas kernels, attention_grads(): pl.pallas_call(functools.partial(compute_kernel, spans), out_shape=(jax.S...  120 us
    ppermute x1, waiting for transfers between devices, per_device(): dq = jnp.concatenate([dq[0], lax.ppermute(dq[1], 'span', swap)], axis=0)  58.4 us
    all_gather x1, waiting for transfers between devices, per_device(): kv = lax.all_gather(kv, 'span', axis=0, tiled=True)  19.6 us
    all_to_all x1, waiting for transfers between devices, per_device(): qdo = lax.all_to_all(qdo, 'seq', split_axis=0, concat_axis=2, tiled=True)[0]  12 us
    all_to_all x1, blocking collectives, per_device(): kv = lax.all_to_all(kv, 'seq', split_axis=0, concat_axis=1, tiled=True)[0]  11.4 us
    all_to_all x1, blocking collectives, per_device(): lax.all_to_all(delta, 'seq', split_axis=0, concat_axis=2, tiled=True)[0]  8.45 us
    unnamed x13, local copies, waits for them, and re-layouts  7.47 us
    all_to_all x1, starting transfers between devices, per_device(): dkv = lax.all_to_all(dkv, 'span', split_axis=1, concat_axis=1, tiled=True)  6.46 us
  transfers between devices with their start and end apart: 8, of which 6 were waited for; matrix products, arithmetic and copies ran while one was open for 4% of the time, Pallas kernels for 0%

profile of v1, /device:TPU:99, one launch (start us, length us, event | category | flops | bytes accessed | tf_op | source)
XLA Modules:
  0.0 303.5 jit_solution(4025039760013544878)
XLA Ops:
  7.2 0.0 copy-start.1
  7.2 0.0 all-gather.2.cloned.1.call-start
  7.2 1.1 copy.41
  8.3 1.0 copy.42
  9.3 11.4 %all_to_all.77 = bf16[8,128,128]{1,2,0:T(8,128)(2,1)S(1)} all-to-all(bf16[8,128,128]{1,2,0:T(8,128)(2,1)S(1)} %maximum_bitcast_fusion.2), channel_id=1, replica_groups=mesh['seq'=8,'span'=16] {'seq'}, dimensions={0} | all-to-all | bytes 524288 | tf_op jit(solution)/shard_map/all_to_all | solution.py:191
  20.8 0.8 copy.43
  21.6 0.0 all-gather.2.cloned.1.call-update
  21.6 1.2 copy.37
  22.9 1.2 copy.38
  24.1 1.0 maximum_bitcast_fusion
  25.1 4.5 %all-to-all-start = ((bf16[8,3,128,128]{2,3,1,0:T(8,128)(2,1)}), bf16[8,3,128,128]{2,3,1,0:T(8,128)(2,1)S(1)}, u32[]{:S(2)}, u32[]{:S(2)}) async-start(bf16[8,3,128,128]{2,3,1,0:T(8,128)(2,1)} %maximum_bitcast_fusion), calls=%async_computation | async-start | bytes 1572864 | tf_op jit(solution)/shard_map/all_to_all | solution.py:189
  29.5 0.0 copy-done.1
  29.5 0.2 copy.40
  29.8 12.0 %all-to-all-done = bf16[8,3,128,128]{2,3,1,0:T(8,128)(2,1)S(1)} async-done(((bf16[8,3,128,128]{2,3,1,0:T(8,128)(2,1)}), bf16[8,3,128,128]{2,3,1,0:T(8,128)(2,1)S(1)}, u32[]{:S(2)}, u32[]{:S(2)}) %all-to-all-start) | async-done | bytes 786464 | tf_op jit(solution)/shard_map/all_to_all | solution.py:189
  41.7 0.4 copy.39
  42.1 0.1 slice_bitcast_fusion
  42.2 0.1 collective-permute-start
  42.3 0.2 fusion
  42.4 8.5 %all_to_all.78 = f32[8,8,128]{2,1,0:T(8,128)S(1)} all-to-all(f32[8,8,128]{2,1,0:T(8,128)S(1)} %pad.4), channel_id=1, replica_groups=mesh['seq'=8,'span'=16] {'seq'}, dimensions={0} | all-to-all | bytes 65536 | tf_op jit(solution)/shard_map/all_to_all | solution.py:190
  50.9 3.7 %collective-permute-start.1 = (f32[8,512]{1,0:T(8,128)S(1)}, f32[8,512]{1,0:T(8,128)S(1)}, u32[]{:S(2)}, u32[]{:S(2)}) collective-permute-start(f32[8,512]{1,0:T(8,128)S(1)} %get-tuple-element.23), channel_id=1, source_target_pairs={{0,15},{1,14},{2,13},{3,12},{4,11},{5,10},{6,9},{7,8},{8,7},{9,6},... | collective-permute-start | bytes 49160 | tf_op jit(solution)/shard_map/ppermute | solution.py:194
  54.6 1.1 collective-permute-done.1
  55.8 0.6 pad_maximum_fusion.1.delta_ref
  56.4 0.0 collective-permute-done
  56.4 1.0 pad_maximum_fusion.qdo_ref
  57.3 19.6 %all-gather.2.cloned.1.call-done.kv_ref = bf16[16384,128]{1,0:T(8,128)(2,1)} async-done(((bf16[1024,128]{1,0:T(8,128)(2,1)}), bf16[16384,128]{1,0:T(8,128)(2,1)}) %all-gather.2.cloned.1.call-update) | async-done | bytes 4194320 | tf_op jit(solution)/shard_map/all_gather | solution.py:192
  76.9 120.3 %attention_grads.1 = (bf16[2,1536,128]{2,1,0:T(8,128)(2,1)}, f32[128,16384]{1,0:T(8,128)}) custom-call(bf16[2,3,512,128]{3,2,1,0:T(8,128)(2,1)} %pad_maximum_fusion.qdo_ref, f32[2,8,512]{2,1,0:T(8,128)} %pad_maximum_fusion.1.delta_ref, bf16[16384,128]{1,0:T(8,128)(2,1)} %all-gather.2.cloned.1.call-done.kv_ref), custom_call_target="tpu_custom_call" | custom-call | tf_op jit(solution)/shard_map/attention_grads/pallas_call | solution.py:143
  197.2 3.9 %convert_element_type.27 = bf16[128,16384]{1,0:T(8,128)(2,1)S(1)} convert(f32[128,16384]{1,0:T(8,128)} %get-tuple-element.6) | non-fusion elementwise | flops 2097152 | bytes 12582912 | tf_op jit(solution)/shard_map/convert_element_type | solution.py:198
  201.1 2.4 copy.59
  203.5 0.0 copy-start
  203.5 6.5 %all-to-all-start.4 = ((bf16[128,16,1024]{2,0,1:T(8,128)(2,1)}), bf16[128,16,1024]{2,0,1:T(8,128)(2,1)}, u32[]{:S(2)}, u32[]{:S(2)}) async-start(bf16[128,16,1024]{2,0,1:T(8,128)(2,1)} %bitcast.56), calls=%async_computation.4 | async-start | bytes 8388608 | tf_op jit(solution)/shard_map/all_to_all | solution.py:199
  210.0 0.0 copy-done
  210.0 0.3 copy.54
  210.3 1.3 collective-permute-start.2
  211.6 58.4 %collective-permute-done.2 = bf16[512,192]{0,1:T(8,128)(2,1)S(1)} collective-permute-done((bf16[512,192]{0,1:T(8,128)(2,1)S(1)}, bf16[512,192]{0,1:T(8,128)(2,1)S(1)}, u32[]{:S(2)}, u32[]{:S(2)}) %collective-permute-start.2) | collective-permute-done | bytes 196640 | tf_op jit(solution)/shard_map/ppermute | solution.py:206
  270.0 0.8 copy_bitcast_fusion.1
  270.8 0.0 all-to-all-done.4
  270.8 5.4 %all-to-all-start.3 = ((bf16[8,128,192]{1,2,0:T(8,128)(2,1)}), bf16[8,128,192]{1,2,0:T(8,128)(2,1)S(1)}, u32[]{:S(2)}, u32[]{:S(2)}) async-start(bf16[8,128,192]{1,2,0:T(8,128)(2,1)} %copy_bitcast_fusion.1), calls=%async_computation.3 | async-start | bytes 786432 | tf_op jit(solution)/shard_map/all_to_all | solution.py:207
  276.2 3.1 %reduce_sum.22 = bf16[128,1024]{1,0:T(8,128)(2,1)S(1)} reduce(bf16[128,16,1024]{2,0,1:T(8,128)(2,1)} %all-to-all-done.4, bf16[]{:T(256)} %constant.5.clone.1), dimensions={1}, to_apply=%region_1.2 | reduce | flops 1966080 | bytes 4456450 | tf_op jit(solution)/shard_map/reduce_sum | solution.py:200
  279.3 0.8 copy.48
  280.2 3.7 %all-to-all-done.3 = bf16[8,128,192]{1,2,0:T(8,128)(2,1)S(1)} async-done(((bf16[8,128,192]{1,2,0:T(8,128)(2,1)}), bf16[8,128,192]{1,2,0:T(8,128)(2,1)S(1)}, u32[]{:S(2)}, u32[]{:S(2)}) %all-to-all-start.3) | async-done | bytes 393248 | tf_op jit(solution)/shard_map/all_to_all | solution.py:207
  283.9 4.5 %all-to-all-start.5 = ((bf16[8,128,128]{2,1,0:T(8,128)(2,1)}), bf16[8,128,128]{2,1,0:T(8,128)(2,1)S(1)}, u32[]{:S(2)}, u32[]{:S(2)}) async-start(bf16[8,128,128]{2,1,0:T(8,128)(2,1)} %bitcast.29), calls=%async_computation.5 | async-start | bytes 524288 | tf_op jit(solution)/shard_map/all_to_all | solution.py:202
  288.4 0.9 copy.50
  289.4 5.6 %all-to-all-done.5 = bf16[8,128,128]{2,1,0:T(8,128)(2,1)S(1)} async-done(((bf16[8,128,128]{2,1,0:T(8,128)(2,1)}), bf16[8,128,128]{2,1,0:T(8,128)(2,1)S(1)}, u32[]{:S(2)}, u32[]{:S(2)}) %all-to-all-start.5) | async-done | bytes 262176 | tf_op jit(solution)/shard_map/all_to_all | solution.py:202
  294.9 0.2 copy.49
  295.2 0.8 copy.52
  295.9 0.8 copy.51
  (5 shorter events, 0.1 us)
Async XLA Ops:
  7.2 22.4 %copy-start.1 = (bf16[1,128,1536]{2,1,0:T(8,128)(2,1)S(1)}, bf16[1,128,1536]{2,1,0:T(8,128)(2,1)}, u32[]{:S(2)}) copy-start(bf16[1,128,1536]{2,1,0:T(8,128)(2,1)} %param.8) | copy-start | bytes 1179652
  7.2 69.7 %all-gather.2.cloned.1.call-start = ((), (), s32[]{:S(2)}) async-start(), calls=%async_computation.6 | async-start | bytes 4456448 | tf_op jit(solution)/shard_map/all_gather | solution.py:192
  25.1 16.7 %all-to-all-start = ((bf16[8,3,128,128]{2,3,1,0:T(8,128)(2,1)}), bf16[8,3,128,128]{2,3,1,0:T(8,128)(2,1)S(1)}, u32[]{:S(2)}, u32[]{:S(2)}) async-start(bf16[8,3,128,128]{2,3,1,0:T(8,128)(2,1)} %maximum_bitcast_fusion), calls=%async_computation | async-start | bytes 1572864 | tf_op jit(solution)/shard_map/all_to_all | solution.py:189
  42.2 14.2 %collective-permute-start = (bf16[3,512,128]{2,1,0:T(8,128)(2,1)S(1)}, bf16[3,512,128]{2,1,0:T(8,128)(2,1)S(1)}, u32[]{:S(2)}, u32[]{:S(2)}) collective-permute-start(bf16[3,512,128]{2,1,0:T(8,128)(2,1)S(1)} %get-tuple-element.17), channel_id=1, source_target_pairs={{0,15},{1,14},{2,13},{3,12},{4,11},{5,10},{6,9},{7,8},{8,7},{9,6},... | collective-permute-start | bytes 1179656 | tf_op jit(solution)/shard_map/ppermute | solution.py:193
  50.9 4.9 %collective-permute-start.1 = (f32[8,512]{1,0:T(8,128)S(1)}, f32[8,512]{1,0:T(8,128)S(1)}, u32[]{:S(2)}, u32[]{:S(2)}) collective-permute-start(f32[8,512]{1,0:T(8,128)S(1)} %get-tuple-element.23), channel_id=1, source_target_pairs={{0,15},{1,14},{2,13},{3,12},{4,11},{5,10},{6,9},{7,8},{8,7},{9,6},... | collective-permute-start | bytes 49160 | tf_op jit(solution)/shard_map/ppermute | solution.py:194
  203.5 6.5 %copy-start = (bf16[2,1536,128]{2,1,0:T(8,128)(2,1)S(1)}, bf16[2,1536,128]{2,1,0:T(8,128)(2,1)}, u32[]{:S(2)}) copy-start(bf16[2,1536,128]{2,1,0:T(8,128)(2,1)} %get-tuple-element.5) | copy-start | bytes 2359300
  203.5 67.2 %all-to-all-start.4 = ((bf16[128,16,1024]{2,0,1:T(8,128)(2,1)}), bf16[128,16,1024]{2,0,1:T(8,128)(2,1)}, u32[]{:S(2)}, u32[]{:S(2)}) async-start(bf16[128,16,1024]{2,0,1:T(8,128)(2,1)} %bitcast.56), calls=%async_computation.4 | async-start | bytes 8388608 | tf_op jit(solution)/shard_map/all_to_all | solution.py:199
  210.3 59.7 %collective-permute-start.2 = (bf16[512,192]{0,1:T(8,128)(2,1)S(1)}, bf16[512,192]{0,1:T(8,128)(2,1)S(1)}, u32[]{:S(2)}, u32[]{:S(2)}) collective-permute-start(bf16[512,192]{0,1:T(8,128)(2,1)S(1)} %bitcast.75), channel_id=1, source_target_pairs={{0,15},{1,14},{2,13},{3,12},{4,11},{5,10},{6,9},{7,8},{8,7},{9,6},... | collective-permute-start | bytes 589832 | tf_op jit(solution)/shard_map/ppermute | solution.py:206
  270.8 13.1 %all-to-all-start.3 = ((bf16[8,128,192]{1,2,0:T(8,128)(2,1)}), bf16[8,128,192]{1,2,0:T(8,128)(2,1)S(1)}, u32[]{:S(2)}, u32[]{:S(2)}) async-start(bf16[8,128,192]{1,2,0:T(8,128)(2,1)} %copy_bitcast_fusion.1), calls=%async_computation.3 | async-start | bytes 786432 | tf_op jit(solution)/shard_map/all_to_all | solution.py:207
  283.9 11.0 %all-to-all-start.5 = ((bf16[8,128,128]{2,1,0:T(8,128)(2,1)}), bf16[8,128,128]{2,1,0:T(8,128)(2,1)S(1)}, u32[]{:S(2)}, u32[]{:S(2)}) async-start(bf16[8,128,128]{2,1,0:T(8,128)(2,1)} %bitcast.29), calls=%async_computation.5 | async-start | bytes 524288 | tf_op jit(solution)/shard_map/all_to_all | solution.py:202
Sparse Core Ops, SparseCore 0:
  21.8 55.0 all-gather.1

commit v2 on v1

v2 whole, which is shorter than its diff:
```python
import functools
import math

import jax
import jax.numpy as jnp
from jax import lax
from jax.experimental import pallas as pl
from jax.experimental.pallas import tpu as pltpu
from jax.sharding import PartitionSpec as P

HEAD_WIDTH = 64
QUERY_PER_KEY = 3
TILE = 512
CHUNK = 256
LANES = 128
NEG_LARGE = -1e30
SCORE_SCALE = 1.0 / math.sqrt(HEAD_WIDTH)
BASE2_SCALE = SCORE_SCALE * math.log2(math.e)
F32 = jnp.float32
BF16 = jnp.bfloat16


def dot(a, b, contract):
    return lax.dot_general(a, b, ((contract[0], contract[1]), ((), ())), preferred_element_type=F32)


def three_parts(x):
    first = x.astype(BF16).astype(F32)
    rest = x - first
    second = rest.astype(BF16).astype(F32)
    return first, second, rest - second


def fused_kernel(seqs, spans, q_in, k_in, v_in, o_in, do_in, qg_out, kg_out, vg_out, kv, qdo, delta, lt, l2, ks1, ks2, vs1, stat_m, stat_l,
                 dq_acc, p_buf, ds_buf, dkv_acc, kv_send, qdo_send, delta_send, part_send, part_recv, dq_send, dq_recv, grad_send, grad_recv,
                 kv_ss, kv_rs, qdo_ss, qdo_rs, delta_ss, delta_rs, cast_ss, cast_rs, part_ss, part_rs, dq_ss, dq_rs, grad_ss, grad_rs):
    own = lax.axis_index("span")
    seq = lax.axis_index("seq")
    tokens = q_in.shape[1]
    block_len = tokens * seqs
    half = seqs // 2
    rows = QUERY_PER_KEY * TILE
    key_tiles = kv.shape[0] // TILE
    mirror = spans - 1 - own
    unit = lax.div(seq, half)
    unit_span = jnp.where(unit == 0, own, mirror)
    unit_piece = lax.rem(seq, half)

    def needs(span, block):
        return block <= jnp.maximum(span, spans - 1 - span)

    def shifted(k, sign):
        z_step = lax.rem(k, 4)
        x_step = lax.rem(lax.div(k, 4) + z_step, 4)
        x = lax.rem(lax.div(own, 4) + 4 + sign * x_step, 4)
        z = lax.rem(lax.rem(own, 4) + 4 + sign * z_step, 4)
        return x * 4 + z

    def seq_shifted(k, sign):
        return lax.rem(seq + seqs + sign * k, seqs)

    def remote(source, target, send, receive, span, at_seq):
        return pltpu.make_async_remote_copy(
            src_ref=source, dst_ref=target, send_sem=send, recv_sem=receive,
            device_id={"span": span, "seq": at_seq}, device_id_type=pl.DeviceIdType.MESH,
        )

    barrier = pltpu.get_barrier_semaphore()

    def greet(span, at_seq):
        pl.semaphore_signal(barrier, inc=1, device_id={"span": span, "seq": at_seq}, device_id_type=pl.DeviceIdType.MESH)

    for k in range(1, seqs):
        greet(own, seq_shifted(k, 1))
    for k in range(seqs):
        greet(mirror, seq_shifted(k, 1))

    @pl.loop(1, spans)
    def _(k):
        there = shifted(k, 1)

        @pl.when(there != mirror)
        def _():
            greet(there, seq)

    lane = lax.broadcasted_iota(jnp.int32, (tokens, LANES), 1)
    low = lane < HEAD_WIDTH

    def columns(ref, i):
        return ref[0, :, i * LANES : (i + 1) * LANES].astype(F32)

    def paired(a, b):
        return (
            jnp.where(low, a, pltpu.roll(b, HEAD_WIDTH, 1)).astype(BF16),
            jnp.where(low, pltpu.roll(a, HEAD_WIDTH, 1), b).astype(BF16),
        )

    for i in range(seqs // 2):
        kv_send[2 * i], kv_send[2 * i + 1] = paired(columns(k_in, i), columns(v_in, i))

    pl.semaphore_wait(barrier, (seqs - 1) + seqs + (spans - 2))

    def kv_copy(k):
        there = seq_shifted(k, 1)
        at = pl.ds(pl.multiple_of(own * block_len + seq * tokens, tokens), tokens)
        return remote(kv_send.at[there], kv.at[at], kv_ss.at[k], kv_rs.at[k], own, there)

    for k in range(1, seqs):
        kv_copy(k).start()
    kv[pl.ds(pl.multiple_of(own * block_len + seq * tokens, tokens), tokens), :] = kv_send[seq]

    heads = seqs * QUERY_PER_KEY
    for i in range(heads // 2):
        a, b = paired(columns(q_in, i), columns(do_in, i))
        n = 2 * i
        qdo_send[n // QUERY_PER_KEY, n % QUERY_PER_KEY] = a
        n = 2 * i + 1
        qdo_send[n // QUERY_PER_KEY, n % QUERY_PER_KEY] = b

    def qdo_copy(k):
        there = seq_shifted(k, 1)
        at = pl.ds(pl.multiple_of(unit_piece * tokens, tokens), tokens)
        return remote(qdo_send.at[there], qdo.at[unit, :, at, :], qdo_ss.at[k], qdo_rs.at[k], unit_span, there)

    def delta_copy(k):
        there = seq_shifted(k, 1)
        return remote(
            delta_send.at[pl.ds(pl.multiple_of(there * 8, 8), 8), :], delta.at[unit, unit_piece],
            delta_ss.at[k], delta_rs.at[k], unit_span, there,
        )

    for k in range(1, seqs):
        qdo_copy(k).start()

    @pl.when(unit == 0)
    def _():
        qdo[0, :, pl.ds(pl.multiple_of(unit_piece * tokens, tokens), tokens), :] = qdo_send[seq]

    @pl.when(unit != 0)
    def _():
        qdo_copy(0).start()

    for k in range(1, seqs):
        kv_copy(k).wait_recv()

    def cast_copy(k):
        at = pl.ds(pl.multiple_of(own * block_len, block_len), block_len)
        return remote(kv.at[at], kv.at[at], cast_ss.at[k], cast_rs.at[k], shifted(k, 1), seq)

    def cast_wait(k):
        at = pl.ds(pl.multiple_of(shifted(k, -1) * block_len, block_len), block_len)
        remote(kv.at[at], kv.at[at], cast_ss.at[k], cast_rs.at[k], shifted(k, 1), seq).wait_recv()

    @pl.loop(1, spans)
    def _(k):
        @pl.when(needs(shifted(k, 1), own))
        def _():
            cast_copy(k).start()

    head_row = lax.broadcasted_iota(jnp.int32, (8 * seqs, heads * HEAD_WIDTH), 0)
    head_col = lax.broadcasted_iota(jnp.int32, (8 * seqs, heads * HEAD_WIDTH), 1)
    in_group = head_row - lax.shift_left(lax.shift_right_logical(head_row, 3), 3)
    wanted = lax.shift_right_logical(head_row, 3) * QUERY_PER_KEY + in_group
    member = (in_group < QUERY_PER_KEY) & (wanted == lax.shift_right_logical(head_col, 6))
    selector = jnp.where(member, 1.0, 0.0).astype(BF16)
    product = do_in[0].astype(F32) * o_in[0].astype(F32)
    product_high = product.astype(BF16)
    product_low = (product - product_high.astype(F32)).astype(BF16)
    delta_send[...] = dot(selector, product_high, ((1,), (1,))) + dot(selector, product_low, ((1,), (1,)))
    for k in range(1, seqs):
        delta_copy(k).start()

    @pl.when(unit == 0)
    def _():
        delta[0, unit_piece] = delta_send[pl.ds(pl.multiple_of(seq * 8, 8), 8), :]

    @pl.when(unit != 0)
    def _():
        delta_copy(0).start()

    def from_everyone(copies):
        for k in range(1, seqs):
            copies(k).wait_recv()

        @pl.when(unit != 0)
        def _():
            copies(0).wait_recv()

    from_everyone(qdo_copy)

    @pl.loop(0, 2)
    def _(u):
        for h in range(QUERY_PER_KEY):
            cols = pl.ds(h * TILE, TILE)
            turned = qdo[u, h].astype(F32).T
            lt[u, 0:128, cols] = turned.astype(BF16)
            lt[u, 128:256, cols] = jnp.concatenate([turned[0:64], jnp.zeros((64, TILE), F32)], axis=0).astype(BF16)
        dq_acc[u] = jnp.zeros((rows, LANES), F32)
        stat_m[u] = jnp.full((8, rows), NEG_LARGE, F32)
        stat_l[u] = jnp.zeros((8, rows), F32)

    key_lane = lax.broadcasted_iota(jnp.int32, (TILE, LANES), 1)
    aux_s = jnp.where((key_lane >= 64) & (key_lane < 67), -1.0, 0.0)
    aux_v = jnp.where((key_lane >= 67) & (key_lane < 70), -1.0, 0.0).astype(BF16)

    def prepare(t):
        at = pl.ds(pl.multiple_of(t * TILE, TILE), TILE)
        raw = kv[at, :].astype(F32)
        scaled = raw * BASE2_SCALE
        high = scaled.astype(BF16).astype(F32)
        ks1[at, :] = jnp.where(key_lane < 64, high, 0.0).astype(BF16)
        ks2[at, :] = jnp.where(key_lane < 64, scaled - high, aux_s).astype(BF16)
        vs1[at, :] = jnp.where(key_lane >= 64, raw, 0.0).astype(BF16)

    def stats(u, t, masked):
        at = pl.ds(pl.multiple_of(t * TILE, TILE), TILE)
        w = jnp.concatenate([ks1[at, :], ks2[at, :]], axis=1)
        for h in range(QUERY_PER_KEY):
            cols = pl.ds(h * TILE, TILE)
            s = dot(w, lt[u, :, cols], ((1,), (0,)))
            if masked:
                key_at = lax.broadcasted_iota(jnp.int32, (TILE, TILE), 0)
                query_at = lax.broadcasted_iota(jnp.int32, (TILE, TILE), 1)
                s = jnp.where(key_at <= query_at, s, NEG_LARGE)
            old = stat_m[u, 0:1, cols]
            new = jnp.maximum(old, jnp.max(s, axis=0, keepdims=True))
            e = jnp.exp2(s - new)
            part = jnp.sum(e.reshape(TILE // 8, 8, TILE), axis=0)
            stat_l[u, :, cols] = stat_l[u, :, cols] * jnp.exp2(old - new) + part
            stat_m[u, :, cols] = jnp.broadcast_to(new, (8, TILE))

    def visit(block, step):
        @pl.loop(0, 4)
        def _(i):
            u = lax.rem(i, 2)
            t = block * 2 + lax.div(i, 2)
            last = jnp.where(u == 0, 2 * own, key_tiles - 1 - 2 * own)

            @pl.when(t < last)
            def _():
                step(u, t, False)

            @pl.when(t == last)
            def _():
                step(u, t, True)

    @pl.loop(0, spans)
    def _(k):
        block = shifted(k, -1)

        @pl.when(needs(own, block))
        def _():
            @pl.when(k > 0)
            def _():
                cast_wait(k)

            prepare(2 * block)
            prepare(2 * block + 1)
            visit(block, stats)

    from_everyone(delta_copy)
    row = lax.broadcasted_iota(jnp.int32, (16, TILE), 0)

    @pl.loop(0, 2)
    def _(u):
        for h in range(QUERY_PER_KEY):
            cols = pl.ds(h * TILE, TILE)
            total = jnp.sum(stat_l[u, :, cols], axis=0, keepdims=True)
            lse = stat_m[u, 0:1, cols] + jnp.log2(total)
            shifts = jnp.concatenate([delta[u, i, h : h + 1, :] for i in range(half)], axis=1)
            parts = three_parts(lse) + three_parts(shifts)
            block = jnp.zeros((16, TILE), F32)
            for i, part in enumerate(parts):
                block = jnp.where(row == i, part, block)
            lt[u, 192:208, cols] = block.astype(BF16)
            l2[u, h] = lt[u, 128:256, cols].astype(F32).T.astype(BF16)

    def main(u, t, masked):
        at = pl.ds(pl.multiple_of(t * TILE, TILE), TILE)
        within = pl.ds(pl.multiple_of(lax.rem(t, 2) * TILE, TILE), TILE)
        kw = jnp.concatenate([ks1[at, :], ks2[at, :]], axis=1)
        vw = jnp.concatenate([vs1[at, :], aux_v], axis=1)
        raw = kv[at, :]
        if masked:
            key_col = lax.broadcasted_iota(jnp.int32, (CHUNK, TILE), 1)
            query_row = lax.broadcasted_iota(jnp.int32, (CHUNK, TILE), 0)
        for h in range(QUERY_PER_KEY):
            for first in range(0, TILE, CHUNK):
                here = pl.ds(h * TILE + first, CHUNK)
                lhs = jnp.concatenate([qdo[u, h, first : first + CHUNK, :], l2[u, h, first : first + CHUNK, :]], axis=1)
                s = dot(lhs, kw, ((1,), (1,)))
                dp = dot(lhs, vw, ((1,), (1,)))
                p = jnp.exp2(s)
                if masked:
                    p = jnp.where(key_col <= query_row + first, p, 0.0)
                ds = (p * dp).astype(BF16)
                p_buf[here, :] = p.astype(BF16)
                ds_buf[here, :] = ds
                dq_acc[u, here, :] += dot(ds, raw, ((1,), (0,)))
        dkv_acc[0:64, within] += dot(lt[u, 0:64, :], ds_buf[...], ((1,), (0,)))
        dkv_acc[64:128, within] += dot(lt[u, 64:128, :], p_buf[...], ((1,), (0,)))

    def part_copy(k):
        return remote(part_send.at[k], part_recv.at[k], part_ss.at[k], part_rs.at[k], shifted(k, -1), seq)

    @pl.loop(1, spans + 1)
    def _(j):
        k = lax.rem(j, spans)
        block = shifted(k, -1)

        @pl.when(needs(own, block))
        def _():
            dkv_acc[...] = jnp.zeros((LANES, block_len), F32)
            visit(block, main)
            dkv_acc[0:64, :] = dkv_acc[0:64, :] * SCORE_SCALE

            @pl.when(k > 0)
            def _():
                part_send[k] = dkv_acc[...].astype(BF16)
                part_copy(k).start()

    even = lax.rem(seq, 2) == 0

    def dq_copy(j):
        u, i = j // half, j % half
        at_span = own if u == 0 else mirror
        return remote(dq_send.at[j], dq_recv.at[seq], dq_ss.at[j], dq_rs.at[seq], at_span, j)

    def dq_arrival(g):
        return remote(dq_send.at[0], dq_recv.at[g], dq_ss.at[0], dq_rs.at[g], own, g)

    for j in range(seqs):
        u, i = j // half, j % half
        h0, h1, h2 = (dq_acc[u, h * TILE + i * tokens : h * TILE + (i + 1) * tokens, :] * SCORE_SCALE for h in range(QUERY_PER_KEY))
        middle = pltpu.roll(h1, HEAD_WIDTH, 1)
        first = jnp.where(even, jnp.where(low, h0, middle), pltpu.roll(h0, HEAD_WIDTH, 1))
        second = jnp.where(even, h2, jnp.where(low, h1, pltpu.roll(h2, HEAD_WIDTH, 1)))
        dq_send[j, 0] = first.astype(BF16)
        dq_send[j, 1] = second.astype(BF16)
        if u == 0:
            @pl.when(seq == j)
            def _():
                dq_recv[j] = dq_send[j]

            @pl.when(seq != j)
            def _():
                dq_copy(j).start()
        else:
            dq_copy(j).start()

    @pl.loop(1, spans)
    def _(k):
        @pl.when(needs(shifted(k, 1), own))
        def _():
            part_copy(k).wait_recv()
            dkv_acc[...] += part_recv[k].astype(F32)

    def grad_copy(k):
        there = seq_shifted(k, 1)
        return remote(grad_send.at[k], grad_recv.at[k], grad_ss.at[k], grad_rs.at[k], own, there)

    for k in range(seqs):
        there = seq_shifted(k, 1)
        piece = dkv_acc[:, pl.ds(pl.multiple_of(there * tokens, tokens), tokens)].T.astype(BF16)
        if k == 0:
            grad_recv[0] = piece
        else:
            grad_send[k] = piece
            grad_copy(k).start()

    for g in range(seqs):
        remote_here = jnp.logical_or(unit != 0, seq != g)

        @pl.when(remote_here)
        def _():
            dq_arrival(g).wait_recv()

    for i in range(seqs // 2):
        at = 3 * LANES * i
        qg_out[0, :, at : at + LANES] = dq_recv[2 * i, 0]
        both = jnp.where(low, dq_recv[2 * i, 1].astype(F32), dq_recv[2 * i + 1, 0].astype(F32))
        qg_out[0, :, at + LANES : at + 2 * LANES] = both.astype(BF16)
        qg_out[0, :, at + 2 * LANES : at + 3 * LANES] = dq_recv[2 * i + 1, 1]

    for k in range(1, seqs):
        grad_copy(k).wait_recv()
    for i in range(seqs // 2):
        a = grad_recv[lax.rem(seq + seqs - 2 * i, seqs)]
        b = grad_recv[lax.rem(seq + seqs - 2 * i - 1, seqs)]
        key_part, value_part = paired(a.astype(F32), b.astype(F32))
        kg_out[0, :, i * LANES : (i + 1) * LANES] = key_part
        vg_out[0, :, i * LANES : (i + 1) * LANES] = value_part

    for k in range(1, seqs):
        kv_copy(k).wait_send()
        qdo_copy(k).wait_send()
        delta_copy(k).wait_send()
        grad_copy(k).wait_send()

    @pl.when(unit != 0)
    def _():
        qdo_copy(0).wait_send()
        delta_copy(0).wait_send()

    for j in range(seqs):
        if j < half:
            @pl.when(seq != j)
            def _():
                dq_copy(j).wait_send()
        else:
            dq_copy(j).wait_send()

    @pl.loop(1, spans)
    def _(k):
        @pl.when(needs(shifted(k, 1), own))
        def _():
            cast_copy(k).wait_send()

        @pl.when(needs(own, shifted(k, -1)))
        def _():
            part_copy(k).wait_send()


def solution(mesh):
    seqs, spans = mesh.shape["seq"], mesh.shape["span"]
    spec = P("span", "seq", None)

    def per_device(queries, keys, values, attn_output, out_grad):
        tokens = queries.shape[1]
        block_len = tokens * seqs
        total = block_len * spans
        rows = QUERY_PER_KEY * TILE
        vmem = pl.BlockSpec(memory_space=pltpu.VMEM)
        dma = pltpu.SemaphoreType.DMA
        return pl.pallas_call(
            functools.partial(fused_kernel, seqs, spans),
            out_shape=(
                jax.ShapeDtypeStruct(queries.shape, BF16),
                jax.ShapeDtypeStruct(keys.shape, BF16),
                jax.ShapeDtypeStruct(values.shape, BF16),
            ),
            in_specs=[vmem] * 5,
            out_specs=(vmem,) * 3,
            scratch_shapes=[
                pltpu.VMEM((total, LANES), BF16),
                pltpu.VMEM((2, QUERY_PER_KEY, TILE, LANES), BF16),
                pltpu.VMEM((2, seqs // 2, 8, tokens), F32),
                pltpu.VMEM((2, 256, rows), BF16),
                pltpu.VMEM((2, QUERY_PER_KEY, TILE, LANES), BF16),
                pltpu.VMEM((total, LANES), BF16),
                pltpu.VMEM((total, LANES), BF16),
                pltpu.VMEM((total, LANES), BF16),
                pltpu.VMEM((2, 8, rows), F32),
                pltpu.VMEM((2, 8, rows), F32),
                pltpu.VMEM((2, rows, LANES), F32),
                pltpu.VMEM((rows, TILE), BF16),
                pltpu.VMEM((rows, TILE), BF16),
                pltpu.VMEM((LANES, block_len), F32),
                pltpu.VMEM((seqs, tokens, LANES), BF16),
                pltpu.VMEM((seqs, QUERY_PER_KEY, tokens, LANES), BF16),
                pltpu.VMEM((8 * seqs, tokens), F32),
                pltpu.VMEM((spans, LANES, block_len), BF16),
                pltpu.VMEM((spans, LANES, block_len), BF16),
                pltpu.VMEM((seqs, 2, tokens, LANES), BF16),
                pltpu.VMEM((seqs, 2, tokens, LANES), BF16),
                pltpu.VMEM((seqs, tokens, LANES), BF16),
                pltpu.VMEM((seqs, tokens, LANES), BF16),
            ]
            + [dma((seqs,))] * 6 + [dma((spans,))] * 4 + [dma((seqs,))] * 4,
            compiler_params=pltpu.CompilerParams(
                vmem_limit_bytes=60 * 1024 * 1024, collective_id=0, has_side_effects=True
            ),
            name="attention_grads",
        )(queries, keys, values, attn_output, out_grad)

    return jax.shard_map(
        per_device, mesh=mesh, in_specs=(spec,) * 5, out_specs=(spec,) * 3, check_vma=False
    )
```

time: 309 us -> 195 us (0.63)
  the two profiles are of different devices: /device:TPU:99 before, /device:TPU:3 now
where the time goes in v2:
time: 195 us
  Pallas kernels  191 us (98%)
  local copies, waits for them, and re-layouts  3.41 us (2%)
    pallas_call x1, Pallas kernels, per_device(): pl.pallas_call(functools.partial(fused_kernel, seqs, spans), out_shape=(j...  191 us

profile of v2, /device:TPU:3, one launch (start us, length us, event | category | flops | bytes accessed | tf_op | source)
XLA Modules:
  0.0 195.0 jit_solution(13741395067122805882)
XLA Ops:
  0.6 190.9 %attention_grads.1 = (bf16[1,128,1536]{2,1,0:T(8,128)(2,1)}, bf16[1,128,512]{2,1,0:T(8,128)(2,1)}, bf16[1,128,512]{2,1,0:T(8,128)(2,1)}) custom-call(bf16[1,128,1536]{2,1,0:T(8,128)(2,1)} %q_in.1, bf16[1,128,512]{2,1,0:T(8,128)(2,1)} %k_in.1, bf16[1,128,512]{2,1,0:T(8,128)(2,1)} %v_in.1, bf16[1,128,1536]{2,1,0:T(8,128)(2,1)} %o_in.1, bf16[1,128,1536]{2,1,0:T(8,128)(2,1)} %do_in.1), custom_call_target="tpu_custom_call" | custom-call | tf_op jit(solution)/shard_map/attention_grads/pallas_call | solution.py:435
  191.6 0.0 copy-start.1
  191.6 1.8 copy.11
  193.4 0.0 copy-done.1
  193.4 0.0 copy-start
  193.4 0.7 copy.12
  194.1 0.3 copy-done
  194.4 0.7 copy.13
Async XLA Ops:
  191.6 1.8 copy-start.1
  193.4 1.0 copy-start

commit v3 on v2

--- a/solution.py
+++ b/solution.py
@@ -11,7 +11,7 @@
 HEAD_WIDTH = 64
 QUERY_PER_KEY = 3
 TILE = 512
-CHUNK = 256
+HALF = TILE // 2
 LANES = 128
 NEG_LARGE = -1e30
 SCORE_SCALE = 1.0 / math.sqrt(HEAD_WIDTH)
@@ -31,16 +31,18 @@
     return first, second, rest - second
 
 
-def fused_kernel(seqs, spans, q_in, k_in, v_in, o_in, do_in, qg_out, kg_out, vg_out, kv, qdo, delta, lt, l2, ks1, ks2, vs1, stat_m, stat_l,
-                 dq_acc, p_buf, ds_buf, dkv_acc, kv_send, qdo_send, delta_send, part_send, part_recv, dq_send, dq_recv, grad_send, grad_recv,
-                 kv_ss, kv_rs, qdo_ss, qdo_rs, delta_ss, delta_rs, cast_ss, cast_rs, part_ss, part_rs, dq_ss, dq_rs, grad_ss, grad_rs):
+def fused_kernel(seqs, spans, q_in, k_in, v_in, o_in, do_in, qg_out, kg_out, vg_out, k_got, v_got, q_got, do_got, delta, lt, l1, l2, k_rows,
+                 ks_t, vs_t, ks, stat_m, stat_l, dq_acc, p_buf, ds_buf, dkv_acc, k_send, v_send, q_send, do_send, delta_send,
+                 part_send, part_recv, dq_send, dq_recv, grad_send, grad_recv, k_ss, k_rs, v_ss, v_rs, q_ss, q_rs, do_ss, do_rs,
+                 delta_ss, delta_rs, kcast_ss, kcast_rs, vcast_ss, vcast_rs, part_ss, part_rs, dq_ss, dq_rs, grad_ss, grad_rs):
     own = lax.axis_index("span")
     seq = lax.axis_index("seq")
     tokens = q_in.shape[1]
     block_len = tokens * seqs
     half = seqs // 2
     rows = QUERY_PER_KEY * TILE
-    key_tiles = kv.shape[0] // TILE
+    key_tiles = k_rows.shape[0] // TILE
+    packed = tokens // 2
     mirror = spans - 1 - own
     unit = lax.div(seq, half)
     unit_span = jnp.where(unit == 0, own, mirror)
@@ -86,41 +88,52 @@
     lane = lax.broadcasted_iota(jnp.int32, (tokens, LANES), 1)
     low = lane < HEAD_WIDTH
 
-    def columns(ref, i):
-        return ref[0, :, i * LANES : (i + 1) * LANES].astype(F32)
-
     def paired(a, b):
+        mask = lax.broadcasted_iota(jnp.int32, a.shape, 1) < HEAD_WIDTH
         return (
-            jnp.where(low, a, pltpu.roll(b, HEAD_WIDTH, 1)).astype(BF16),
-            jnp.where(low, pltpu.roll(a, HEAD_WIDTH, 1), b).astype(BF16),
+            jnp.where(mask, a, pltpu.roll(b, HEAD_WIDTH, 1)).astype(BF16),
+            jnp.where(mask, pltpu.roll(a, HEAD_WIDTH, 1), b).astype(BF16),
         )
 
-    for i in range(seqs // 2):
-        kv_send[2 * i], kv_send[2 * i + 1] = paired(columns(k_in, i), columns(v_in, i))
-
+    def pack(ref, i):
+        at = slice(i * LANES, (i + 1) * LANES)
+        return paired(ref[0, :packed, at].astype(F32), ref[0, packed:, at].astype(F32))
+
+    heads = seqs * QUERY_PER_KEY
+
+    def pack_keys(ref, out):
+        for i in range(seqs // 2):
+            out[2 * i], out[2 * i + 1] = pack(ref, i)
+
+    def pack_queries(ref, out):
+        for i in range(heads // 2):
+            a, b = pack(ref, i)
+            n = 2 * i
+            out[n // QUERY_PER_KEY, n % QUERY_PER_KEY] = a
+            n = 2 * i + 1
+            out[n // QUERY_PER_KEY, n % QUERY_PER_KEY] = b
+
+    pack_keys(k_in, k_send)
     pl.semaphore_wait(barrier, (seqs - 1) + seqs + (spans - 2))
 
-    def kv_copy(k):
+    own_rows = pl.ds(pl.multiple_of(own * (block_len // 2) + seq * packed, packed), packed)
+    unit_rows = pl.ds(pl.multiple_of(unit_piece * packed, packed), packed)
+
+    def k_copy(k):
         there = seq_shifted(k, 1)
-        at = pl.ds(pl.multiple_of(own * block_len + seq * tokens, tokens), tokens)
-        return remote(kv_send.at[there], kv.at[at], kv_ss.at[k], kv_rs.at[k], own, there)
-
-    for k in range(1, seqs):
-        kv_copy(k).start()
-    kv[pl.ds(pl.multiple_of(own * block_len + seq * tokens, tokens), tokens), :] = kv_send[seq]
-
-    heads = seqs * QUERY_PER_KEY
-    for i in range(heads // 2):
-        a, b = paired(columns(q_in, i), columns(do_in, i))
-        n = 2 * i
-        qdo_send[n // QUERY_PER_KEY, n % QUERY_PER_KEY] = a
-        n = 2 * i + 1
-        qdo_send[n // QUERY_PER_KEY, n % QUERY_PER_KEY] = b
-
-    def qdo_copy(k):
+        return remote(k_send.at[there], k_got.at[own_rows], k_ss.at[k], k_rs.at[k], own, there)
+
+    def v_copy(k):
         there = seq_shifted(k, 1)
-        at = pl.ds(pl.multiple_of(unit_piece * tokens, tokens), tokens)
-        return remote(qdo_send.at[there], qdo.at[unit, :, at, :], qdo_ss.at[k], qdo_rs.at[k], unit_span, there)
+        return remote(v_send.at[there], v_got.at[own_rows], v_ss.at[k], v_rs.at[k], own, there)
+
+    def q_copy(k):
+        there = seq_shifted(k, 1)
+        return remote(q_send.at[there], q_got.at[unit, :, unit_rows, :], q_ss.at[k], q_rs.at[k], unit_span, there)
+
+    def do_copy(k):
+        there = seq_shifted(k, 1)
+        return remote(do_send.at[there], do_got.at[unit, :, unit_rows, :], do_ss.at[k], do_rs.at[k], unit_span, there)
 
     def delta_copy(k):
         there = seq_shifted(k, 1)
@@ -129,33 +142,57 @@
             delta_ss.at[k], delta_rs.at[k], unit_span, there,
         )
 
-    for k in range(1, seqs):
-        qdo_copy(k).start()
+    def cast_copy(k, got, send, receive):
+        at = pl.ds(pl.multiple_of(own * (block_len // 2), block_len // 2), block_len // 2)
+        return remote(got.at[at], got.at[at], send.at[k], receive.at[k], shifted(k, 1), seq)
+
+    def k_cast(k):
+        return cast_copy(k, k_got, kcast_ss, kcast_rs)
+
+    def v_cast(k):
+        return cast_copy(k, v_got, vcast_ss, vcast_rs)
+
+    def cast_all(cast):
+        @pl.loop(1, spans)
+        def _(k):
+            @pl.when(needs(shifted(k, 1), own))
+            def _():
+                cast(k).start()
+
+    for k in range(1, seqs):
+        k_copy(k).start()
+    k_got[own_rows, :] = k_send[seq]
+    pack_queries(q_in, q_send)
+    for k in range(1, seqs):
+        q_copy(k).start()
 
     @pl.when(unit == 0)
     def _():
-        qdo[0, :, pl.ds(pl.multiple_of(unit_piece * tokens, tokens), tokens), :] = qdo_send[seq]
+        q_got[0, :, unit_rows, :] = q_send[seq]
 
     @pl.when(unit != 0)
     def _():
-        qdo_copy(0).start()
-
-    for k in range(1, seqs):
-        kv_copy(k).wait_recv()
-
-    def cast_copy(k):
-        at = pl.ds(pl.multiple_of(own * block_len, block_len), block_len)
-        return remote(kv.at[at], kv.at[at], cast_ss.at[k], cast_rs.at[k], shifted(k, 1), seq)
-
-    def cast_wait(k):
-        at = pl.ds(pl.multiple_of(shifted(k, -1) * block_len, block_len), block_len)
-        remote(kv.at[at], kv.at[at], cast_ss.at[k], cast_rs.at[k], shifted(k, 1), seq).wait_recv()
-
-    @pl.loop(1, spans)
-    def _(k):
-        @pl.when(needs(shifted(k, 1), own))
-        def _():
-            cast_copy(k).start()
+        q_copy(0).start()
+
+    for k in range(1, seqs):
+        k_copy(k).wait_recv()
+    cast_all(k_cast)
+
+    pack_keys(v_in, v_send)
+    for k in range(1, seqs):
+        v_copy(k).start()
+    v_got[own_rows, :] = v_send[seq]
+    pack_queries(do_in, do_send)
+    for k in range(1, seqs):
+        do_copy(k).start()
+
+    @pl.when(unit == 0)
+    def _():
+        do_got[0, :, unit_rows, :] = do_send[seq]
+
+    @pl.when(unit != 0)
+    def _():
+        do_copy(0).start()
 
     head_row = lax.broadcasted_iota(jnp.int32, (8 * seqs, heads * HEAD_WIDTH), 0)
     head_col = lax.broadcasted_iota(jnp.int32, (8 * seqs, heads * HEAD_WIDTH), 1)
@@ -186,42 +223,70 @@
         def _():
             copies(0).wait_recv()
 
-    from_everyone(qdo_copy)
+    from_everyone(q_copy)
+
+    def halves(x):
+        return jnp.concatenate([x[0:HEAD_WIDTH], x[HEAD_WIDTH:]], axis=1)
 
     @pl.loop(0, 2)
     def _(u):
         for h in range(QUERY_PER_KEY):
             cols = pl.ds(h * TILE, TILE)
-            turned = qdo[u, h].astype(F32).T
-            lt[u, 0:128, cols] = turned.astype(BF16)
-            lt[u, 128:256, cols] = jnp.concatenate([turned[0:64], jnp.zeros((64, TILE), F32)], axis=0).astype(BF16)
+            turned = halves(q_got[u, h].astype(F32).T).astype(BF16)
+            nothing = jnp.zeros((HEAD_WIDTH, TILE), BF16)
+            lt[u, 0:64, cols] = turned
+            lt[u, 64:128, cols] = nothing
+            lt[u, 128:192, cols] = turned
+            lt[u, 192:256, cols] = nothing
         dq_acc[u] = jnp.zeros((rows, LANES), F32)
         stat_m[u] = jnp.full((8, rows), NEG_LARGE, F32)
         stat_l[u] = jnp.zeros((8, rows), F32)
 
-    key_lane = lax.broadcasted_iota(jnp.int32, (TILE, LANES), 1)
-    aux_s = jnp.where((key_lane >= 64) & (key_lane < 67), -1.0, 0.0)
-    aux_v = jnp.where((key_lane >= 67) & (key_lane < 70), -1.0, 0.0).astype(BF16)
-
-    def prepare(t):
+    aux_row = lax.broadcasted_iota(jnp.int32, (HEAD_WIDTH, TILE), 0)
+    aux_s = jnp.where(aux_row < 3, -1.0, 0.0)
+    aux_v = jnp.where((aux_row >= 3) & (aux_row < 6), -1.0, 0.0)
+
+    def packed_tile(got, t):
+        return got[pl.ds(pl.multiple_of(t * HALF, HALF), HALF), :].astype(F32)
+
+    def prepare_keys(t):
         at = pl.ds(pl.multiple_of(t * TILE, TILE), TILE)
-        raw = kv[at, :].astype(F32)
+        raw = packed_tile(k_got, t)
+        zero = jnp.zeros((HALF, LANES), F32)
+        mask = lax.broadcasted_iota(jnp.int32, (HALF, LANES), 1) < HEAD_WIDTH
+
+        def spread(x):
+            return jnp.concatenate([jnp.where(mask, x, zero), jnp.where(mask, pltpu.roll(x, HEAD_WIDTH, 1), zero)], axis=0)
+
+        k_rows[at, :] = spread(raw).astype(BF16)
         scaled = raw * BASE2_SCALE
         high = scaled.astype(BF16).astype(F32)
-        ks1[at, :] = jnp.where(key_lane < 64, high, 0.0).astype(BF16)
-        ks2[at, :] = jnp.where(key_lane < 64, scaled - high, aux_s).astype(BF16)
-        vs1[at, :] = jnp.where(key_lane >= 64, raw, 0.0).astype(BF16)
+        rest = scaled - high
+        within = pl.ds(pl.multiple_of(lax.rem(t, 2) * TILE, TILE), TILE)
+        ks[within, 0:128] = spread(high).astype(BF16)
+        ks[within, 128:256] = spread(rest).astype(BF16)
+        nothing = jnp.zeros((HEAD_WIDTH, TILE), F32)
+        ks_t[0:128, at] = jnp.concatenate([halves(high.T), nothing], axis=0).astype(BF16)
+        ks_t[128:256, at] = jnp.concatenate([halves(rest.T), aux_s], axis=0).astype(BF16)
+
+    def prepare_values(t):
+        at = pl.ds(pl.multiple_of(t * TILE, TILE), TILE)
+        nothing = jnp.zeros((HEAD_WIDTH, TILE), F32)
+        vs_t[0:128, at] = jnp.concatenate([nothing, halves(packed_tile(v_got, t).T)], axis=0).astype(BF16)
+        vs_t[128:256, at] = jnp.concatenate([nothing, aux_v], axis=0).astype(BF16)
+
+    def place(axis):
+        r = lax.broadcasted_iota(jnp.int32, (TILE, TILE), axis)
+        quarter = lax.shift_right_logical(r & (HALF - 1), 6)
+        return quarter * 128 + lax.shift_right_logical(r, 8) * 64 + (r & 63)
 
     def stats(u, t, masked):
-        at = pl.ds(pl.multiple_of(t * TILE, TILE), TILE)
-        w = jnp.concatenate([ks1[at, :], ks2[at, :]], axis=1)
+        w = ks[pl.ds(pl.multiple_of(lax.rem(t, 2) * TILE, TILE), TILE), :]
         for h in range(QUERY_PER_KEY):
             cols = pl.ds(h * TILE, TILE)
             s = dot(w, lt[u, :, cols], ((1,), (0,)))
             if masked:
-                key_at = lax.broadcasted_iota(jnp.int32, (TILE, TILE), 0)
-                query_at = lax.broadcasted_iota(jnp.int32, (TILE, TILE), 1)
-                s = jnp.where(key_at <= query_at, s, NEG_LARGE)
+                s = jnp.where(place(0) <= place(1), s, NEG_LARGE)
             old = stat_m[u, 0:1, cols]
             new = jnp.maximum(old, jnp.max(s, axis=0, keepdims=True))
             e = jnp.exp2(s - new)
@@ -244,6 +309,10 @@
             def _():
                 step(u, t, True)
 
+    def cast_wait(k, got, send, receive):
+        at = pl.ds(pl.multiple_of(shifted(k, -1) * (block_len // 2), block_len // 2), block_len // 2)
+        remote(got.at[at], got.at[at], send.at[k], receive.at[k], shifted(k, 1), seq).wait_recv()
+
     @pl.loop(0, spans)
     def _(k):
         block = shifted(k, -1)
@@ -252,13 +321,20 @@
         def _():
             @pl.when(k > 0)
             def _():
-                cast_wait(k)
-
-            prepare(2 * block)
-            prepare(2 * block + 1)
+                cast_wait(k, k_got, kcast_ss, kcast_rs)
+
+            prepare_keys(2 * block)
+            prepare_keys(2 * block + 1)
             visit(block, stats)
 
+            @pl.when(k == 0)
+            def _():
+                for i in range(1, seqs):
+                    v_copy(i).wait_recv()
+                cast_all(v_cast)
+
     from_everyone(delta_copy)
+    from_everyone(do_copy)
     row = lax.broadcasted_iota(jnp.int32, (16, TILE), 0)
 
     @pl.loop(0, 2)
@@ -267,36 +343,35 @@
             cols = pl.ds(h * TILE, TILE)
             total = jnp.sum(stat_l[u, :, cols], axis=0, keepdims=True)
             lse = stat_m[u, 0:1, cols] + jnp.log2(total)
-            shifts = jnp.concatenate([delta[u, i, h : h + 1, :] for i in range(half)], axis=1)
+            pieces = [delta[u, i, h : h + 1, :] for i in range(half)]
+            shifts = jnp.concatenate([x[:, :packed] for x in pieces] + [x[:, packed:] for x in pieces], axis=1)
             parts = three_parts(lse) + three_parts(shifts)
             block = jnp.zeros((16, TILE), F32)
             for i, part in enumerate(parts):
                 block = jnp.where(row == i, part, block)
             lt[u, 192:208, cols] = block.astype(BF16)
+            lt[u, 64:128, cols] = halves(do_got[u, h].astype(F32).T).astype(BF16)
+            l1[u, h, :HALF, :], l1[u, h, HALF:, :] = paired(q_got[u, h].astype(F32), do_got[u, h].astype(F32))
             l2[u, h] = lt[u, 128:256, cols].astype(F32).T.astype(BF16)
 
     def main(u, t, masked):
         at = pl.ds(pl.multiple_of(t * TILE, TILE), TILE)
         within = pl.ds(pl.multiple_of(lax.rem(t, 2) * TILE, TILE), TILE)
-        kw = jnp.concatenate([ks1[at, :], ks2[at, :]], axis=1)
-        vw = jnp.concatenate([vs1[at, :], aux_v], axis=1)
-        raw = kv[at, :]
-        if masked:
-            key_col = lax.broadcasted_iota(jnp.int32, (CHUNK, TILE), 1)
-            query_row = lax.broadcasted_iota(jnp.int32, (CHUNK, TILE), 0)
+        kw = ks_t[:, at]
+        vw = vs_t[:, at]
+        raw = k_rows[at, :]
         for h in range(QUERY_PER_KEY):
-            for first in range(0, TILE, CHUNK):
-                here = pl.ds(h * TILE + first, CHUNK)
-                lhs = jnp.concatenate([qdo[u, h, first : first + CHUNK, :], l2[u, h, first : first + CHUNK, :]], axis=1)
-                s = dot(lhs, kw, ((1,), (1,)))
-                dp = dot(lhs, vw, ((1,), (1,)))
-                p = jnp.exp2(s)
-                if masked:
-                    p = jnp.where(key_col <= query_row + first, p, 0.0)
-                ds = (p * dp).astype(BF16)
-                p_buf[here, :] = p.astype(BF16)
-                ds_buf[here, :] = ds
-                dq_acc[u, here, :] += dot(ds, raw, ((1,), (0,)))
+            here = pl.ds(h * TILE, TILE)
+            lhs = jnp.concatenate([l1[u, h], l2[u, h]], axis=1)
+            s = dot(lhs, kw, ((1,), (0,)))
+            dp = dot(lhs, vw, ((1,), (0,)))
+            p = jnp.exp2(s)
+            if masked:
+                p = jnp.where(place(1) <= place(0), p, 0.0)
+            ds = (p * dp).astype(BF16)
+            p_buf[here, :] = p.astype(BF16)
+            ds_buf[here, :] = ds
+            dq_acc[u, here, :] += dot(ds, raw, ((1,), (0,)))
         dkv_acc[0:64, within] += dot(lt[u, 0:64, :], ds_buf[...], ((1,), (0,)))
         dkv_acc[64:128, within] += dot(lt[u, 64:128, :], p_buf[...], ((1,), (0,)))
 
@@ -310,6 +385,12 @@
 
         @pl.when(needs(own, block))
         def _():
+            @pl.when(k > 0)
+            def _():
+                cast_wait(k, v_got, vcast_ss, vcast_rs)
+
+            prepare_values(2 * block)
+            prepare_values(2 * block + 1)
             dkv_acc[...] = jnp.zeros((LANES, block_len), F32)
             visit(block, main)
             dkv_acc[0:64, :] = dkv_acc[0:64, :] * SCORE_SCALE
@@ -331,7 +412,10 @@
 
     for j in range(seqs):
         u, i = j // half, j % half
-        h0, h1, h2 = (dq_acc[u, h * TILE + i * tokens : h * TILE + (i + 1) * tokens, :] * SCORE_SCALE for h in range(QUERY_PER_KEY))
+        h0, h1, h2 = (
+            jnp.concatenate([dq_acc[u, at : at + packed, :], dq_acc[u, at + HALF : at + HALF + packed, :]], axis=0) * SCORE_SCALE
+            for at in (h * TILE + i * packed for h in range(QUERY_PER_KEY))
+        )
         middle = pltpu.roll(h1, HEAD_WIDTH, 1)
         first = jnp.where(even, jnp.where(low, h0, middle), pltpu.roll(h0, HEAD_WIDTH, 1))
         second = jnp.where(even, h2, jnp.where(low, h1, pltpu.roll(h2, HEAD_WIDTH, 1)))
@@ -357,16 +441,17 @@
 
     def grad_copy(k):
         there = seq_shifted(k, 1)
-        return remote(grad_send.at[k], grad_recv.at[k], grad_ss.at[k], grad_rs.at[k], own, there)
-
-    for k in range(seqs):
-        there = seq_shifted(k, 1)
-        piece = dkv_acc[:, pl.ds(pl.multiple_of(there * tokens, tokens), tokens)].T.astype(BF16)
-        if k == 0:
-            grad_recv[0] = piece
-        else:
-            grad_send[k] = piece
-            grad_copy(k).start()
+        return remote(grad_send.at[there], grad_recv.at[k], grad_ss.at[k], grad_rs.at[k], own, there)
+
+    for j in range(seqs // half):
+        turned = dkv_acc[:, j * TILE : (j + 1) * TILE].T
+        for i in range(half):
+            at = i * packed
+            piece = jnp.concatenate([turned[at : at + packed], turned[at + HALF : at + HALF + packed]], axis=0)
+            grad_send[j * half + i] = piece.astype(BF16)
+    for k in range(1, seqs):
+        grad_copy(k).start()
+    grad_recv[0] = grad_send[seq]
 
     for g in range(seqs):
         remote_here = jnp.logical_or(unit != 0, seq != g)
@@ -392,15 +477,13 @@
         vg_out[0, :, i * LANES : (i + 1) * LANES] = value_part
 
     for k in range(1, seqs):
-        kv_copy(k).wait_send()
-        qdo_copy(k).wait_send()
-        delta_copy(k).wait_send()
-        grad_copy(k).wait_send()
+        for copy in (k_copy, v_copy, q_copy, do_copy, delta_copy, grad_copy):
+            copy(k).wait_send()
 
     @pl.when(unit != 0)
     def _():
-        qdo_copy(0).wait_send()
-        delta_copy(0).wait_send()
+        for copy in (q_copy, do_copy, delta_copy):
+            copy(0).wait_send()
 
     for j in range(seqs):
         if j < half:
@@ -414,7 +497,8 @@
     def _(k):
         @pl.when(needs(shifted(k, 1), own))
         def _():
-            cast_copy(k).wait_send()
+            k_cast(k).wait_send()
+            v_cast(k).wait_send()
 
         @pl.when(needs(own, shifted(k, -1)))
         def _():
@@ -442,22 +526,28 @@
             in_specs=[vmem] * 5,
             out_specs=(vmem,) * 3,
             scratch_shapes=[
-                pltpu.VMEM((total, LANES), BF16),
-                pltpu.VMEM((2, QUERY_PER_KEY, TILE, LANES), BF16),
+                pltpu.VMEM((total // 2, LANES), BF16),
+                pltpu.VMEM((total // 2, LANES), BF16),
+                pltpu.VMEM((2, QUERY_PER_KEY, HALF, LANES), BF16),
+                pltpu.VMEM((2, QUERY_PER_KEY, HALF, LANES), BF16),
                 pltpu.VMEM((2, seqs // 2, 8, tokens), F32),
                 pltpu.VMEM((2, 256, rows), BF16),
                 pltpu.VMEM((2, QUERY_PER_KEY, TILE, LANES), BF16),
+                pltpu.VMEM((2, QUERY_PER_KEY, TILE, LANES), BF16),
                 pltpu.VMEM((total, LANES), BF16),
-                pltpu.VMEM((total, LANES), BF16),
-                pltpu.VMEM((total, LANES), BF16),
+                pltpu.VMEM((256, total), BF16),
+                pltpu.VMEM((256, total), BF16),
+                pltpu.VMEM((2 * TILE, 256), BF16),
                 pltpu.VMEM((2, 8, rows), F32),
                 pltpu.VMEM((2, 8, rows), F32),
                 pltpu.VMEM((2, rows, LANES), F32),
                 pltpu.VMEM((rows, TILE), BF16),
                 pltpu.VMEM((rows, TILE), BF16),
                 pltpu.VMEM((LANES, block_len), F32),
-                pltpu.VMEM((seqs, tokens, LANES), BF16),
-                pltpu.VMEM((seqs, QUERY_PER_KEY, tokens, LANES), BF16),
+                pltpu.VMEM((seqs, tokens // 2, LANES), BF16),
+                pltpu.VMEM((seqs, tokens // 2, LANES), BF16),
+                pltpu.VMEM((seqs, QUERY_PER_KEY, tokens // 2, LANES), BF16),
+                pltpu.VMEM((seqs, QUERY_PER_KEY, tokens // 2, LANES), BF16),
                 pltpu.VMEM((8 * seqs, tokens), F32),
                 pltpu.VMEM((spans, LANES, block_len), BF16),
                 pltpu.VMEM((spans, LANES, block_len), BF16),
@@ -466,7 +556,7 @@
                 pltpu.VMEM((seqs, tokens, LANES), BF16),
                 pltpu.VMEM((seqs, tokens, LANES), BF16),
             ]
-            + [dma((seqs,))] * 6 + [dma((spans,))] * 4 + [dma((seqs,))] * 4,
+            + [dma((seqs,))] * 10 + [dma((spans,))] * 6 + [dma((seqs,))] * 4,
             compiler_params=pltpu.CompilerParams(
                 vmem_limit_bytes=60 * 1024 * 1024, collective_id=0, has_side_effects=True
             ),

time: 195 us -> 164 us (0.84)
  the two profiles are of different devices: /device:TPU:3 before, /device:TPU:99 now
where the time goes in v3:
time: 164 us; the launch traced here: 162 us
  Pallas kernels  158 us (96%)
  local copies, waits for them, and re-layouts  3.41 us (2%)
    pallas_call x1, Pallas kernels, per_device(): pl.pallas_call(functools.partial(fused_kernel, seqs, spans), out_shape=(j...  158 us
    unnamed x7, local copies, waits for them, and re-layouts  3.41 us

profile of v3, /device:TPU:99, one launch (start us, length us, event | category | flops | bytes accessed | tf_op | source)
XLA Modules:
  0.0 161.7 jit_solution(16721972475134015950)
XLA Ops:
  0.6 157.7 %attention_grads.1 = (bf16[1,128,1536]{2,1,0:T(8,128)(2,1)}, bf16[1,128,512]{2,1,0:T(8,128)(2,1)}, bf16[1,128,512]{2,1,0:T(8,128)(2,1)}) custom-call(bf16[1,128,1536]{2,1,0:T(8,128)(2,1)} %q_in.1, bf16[1,128,512]{2,1,0:T(8,128)(2,1)} %k_in.1, bf16[1,128,512]{2,1,0:T(8,128)(2,1)} %v_in.1, bf16[1,128,1536]{2,1,0:T(8,128)(2,1)} %o_in.1, bf16[1,128,1536]{2,1,0:T(8,128)(2,1)} %do_in.1), custom_call_target="tpu_custom_call" | custom-call | tf_op jit(solution)/shard_map/attention_grads/pallas_call | solution.py:519
  158.3 0.0 copy-start.1
  158.3 1.8 %copy.11 = bf16[1,128,1536]{2,1,0:T(8,128)(2,1)} copy(bf16[1,128,1536]{2,1,0:T(8,128)(2,1)} %get-tuple-element.6) | data formatting | bytes 786432
  160.1 0.0 copy-done.1
  160.1 0.0 copy-start
  160.1 0.7 copy.12
  160.8 0.3 copy-done
  161.1 0.7 copy.13
Async XLA Ops:
  158.3 1.8 %copy-start.1 = (bf16[1,128,512]{2,1,0:T(8,128)(2,1)S(1)}, bf16[1,128,512]{2,1,0:T(8,128)(2,1)}, u32[]{:S(2)}) copy-start(bf16[1,128,512]{2,1,0:T(8,128)(2,1)} %get-tuple-element.7) | copy-start | bytes 393220
  160.1 1.0 copy-start

commit v4 on v3

--- a/solution.py
+++ b/solution.py
@@ -12,6 +12,16 @@
 QUERY_PER_KEY = 3
 TILE = 512
 HALF = TILE // 2
+VALUES_AT = 4
+PLACES = (
+    (0, 0), (2, 0), (2, 1), (2, 3), (2, 2), (3, 2), (0, 2), (1, 2),
+    (1, 1), (3, 0), (0, 3), (3, 3), (1, 0), (1, 3), (3, 1), (0, 1),
+)
+VIA = {(2, 2): (1, 2), (2, 0): (1, 0), (2, 1): (3, 1), (2, 3): (3, 3), (1, 2): (1, 3), (3, 2): (3, 1), (0, 2): (0, 1)}
+LAST_RELAYED = 7
+KEYS_ON = ((1, 15), (2, 14), (3, 13), (3, 12), (3, 11), (6, 7))
+VALUES_ON = ((12, 15), (12, 14), (12, 13), (12, 12), (12, 11), (14, 7))
+STRIP = 64
 LANES = 128
 NEG_LARGE = -1e30
 SCORE_SCALE = 1.0 / math.sqrt(HEAD_WIDTH)
@@ -32,7 +42,7 @@
 
 
 def fused_kernel(seqs, spans, q_in, k_in, v_in, o_in, do_in, qg_out, kg_out, vg_out, k_got, v_got, q_got, do_got, delta, lt, l1, l2, k_rows,
-                 ks_t, vs_t, ks, stat_m, stat_l, dq_acc, p_buf, ds_buf, dkv_acc, k_send, v_send, q_send, do_send, delta_send,
+                 ks_t, vs_t, ks, s_buf, stat_m, stat_l, dq_acc, p_buf, ds_buf, dkv_acc, k_send, v_send, q_send, do_send, delta_send,
                  part_send, part_recv, dq_send, dq_recv, grad_send, grad_recv, k_ss, k_rs, v_ss, v_rs, q_ss, q_rs, do_ss, do_rs,
                  delta_ss, delta_rs, kcast_ss, kcast_rs, vcast_ss, vcast_rs, part_ss, part_rs, dq_ss, dq_rs, grad_ss, grad_rs):
     own = lax.axis_index("span")
@@ -51,12 +61,36 @@
     def needs(span, block):
         return block <= jnp.maximum(span, spans - 1 - span)
 
+    def entry(values, k):
+        found = values[0] + 0 * k
+        for i, value in enumerate(values):
+            if value != values[0]:
+                found = jnp.where(k == i, value, found)
+        return found
+
+    def moved(x_step, z_step):
+        x = lax.rem(lax.div(own, 4) + 4 + x_step, 4)
+        z = lax.rem(lax.rem(own, 4) + 4 + z_step, 4)
+        return x * 4 + z
+
     def shifted(k, sign):
-        z_step = lax.rem(k, 4)
-        x_step = lax.rem(lax.div(k, 4) + z_step, 4)
-        x = lax.rem(lax.div(own, 4) + 4 + sign * x_step, 4)
-        z = lax.rem(lax.rem(own, 4) + 4 + sign * z_step, 4)
-        return x * 4 + z
+        return moved(sign * entry([p[0] for p in PLACES], k), sign * entry([p[1] for p in PLACES], k))
+
+    def next_place(p):
+        return VIA.get(p, (0, 0))
+
+    def place_before(k):
+        steps = [[(next_place(p)[axis] - p[axis] + 4) % 4 for p in PLACES] for axis in range(2)]
+        return moved(entry(steps[0], k), entry(steps[1], k))
+
+    def place_after(k):
+        steps = [[(next_place(p)[axis] - p[axis] + 4) % 4 for p in PLACES] for axis in range(2)]
+        return moved(-entry(steps[0], k), -entry(steps[1], k))
+
+    joins = [[PLACES.index(c) for c in PLACES if VIA.get(c) == p] for p in PLACES]
+
+    def joining(k, i):
+        return entry([c[i] if len(c) > i else 0 for c in joins], k)
 
     def seq_shifted(k, sign):
         return lax.rem(seq + seqs + sign * k, seqs)
@@ -84,9 +118,6 @@
         @pl.when(there != mirror)
         def _():
             greet(there, seq)
-
-    lane = lax.broadcasted_iota(jnp.int32, (tokens, LANES), 1)
-    low = lane < HEAD_WIDTH
 
     def paired(a, b):
         mask = lax.broadcasted_iota(jnp.int32, a.shape, 1) < HEAD_WIDTH
@@ -142,9 +173,13 @@
             delta_ss.at[k], delta_rs.at[k], unit_span, there,
         )
 
+    def block_rows(block):
+        return pl.ds(pl.multiple_of(block * (block_len // 2), block_len // 2), block_len // 2)
+
     def cast_copy(k, got, send, receive):
-        at = pl.ds(pl.multiple_of(own * (block_len // 2), block_len // 2), block_len // 2)
-        return remote(got.at[at], got.at[at], send.at[k], receive.at[k], shifted(k, 1), seq)
+        before = entry([PLACES.index(next_place(p)) for p in PLACES], k)
+        at = block_rows(shifted(before, -1))
+        return remote(got.at[at], got.at[at], send.at[k], receive.at[k], place_after(k), seq)
 
     def k_cast(k):
         return cast_copy(k, k_got, kcast_ss, kcast_rs)
@@ -152,12 +187,18 @@
     def v_cast(k):
         return cast_copy(k, v_got, vcast_ss, vcast_rs)
 
+    def pass_on(k, cast):
+        for i in range(max(len(c) for c in joins)):
+            joined = joining(k, i)
+
+            @pl.when(joined > 0)
+            def _():
+                cast(joined).start()
+
     def cast_all(cast):
-        @pl.loop(1, spans)
-        def _(k):
-            @pl.when(needs(shifted(k, 1), own))
-            def _():
-                cast(k).start()
+        @pl.loop(1, spans - LAST_RELAYED)
+        def _(i):
+            cast(spans - i).start()
 
     for k in range(1, seqs):
         k_copy(k).start()
@@ -179,20 +220,7 @@
     cast_all(k_cast)
 
     pack_keys(v_in, v_send)
-    for k in range(1, seqs):
-        v_copy(k).start()
-    v_got[own_rows, :] = v_send[seq]
     pack_queries(do_in, do_send)
-    for k in range(1, seqs):
-        do_copy(k).start()
-
-    @pl.when(unit == 0)
-    def _():
-        do_got[0, :, unit_rows, :] = do_send[seq]
-
-    @pl.when(unit != 0)
-    def _():
-        do_copy(0).start()
 
     head_row = lax.broadcasted_iota(jnp.int32, (8 * seqs, heads * HEAD_WIDTH), 0)
     head_col = lax.broadcasted_iota(jnp.int32, (8 * seqs, heads * HEAD_WIDTH), 1)
@@ -204,16 +232,12 @@
     product_high = product.astype(BF16)
     product_low = (product - product_high.astype(F32)).astype(BF16)
     delta_send[...] = dot(selector, product_high, ((1,), (1,))) + dot(selector, product_low, ((1,), (1,)))
-    for k in range(1, seqs):
-        delta_copy(k).start()
+    v_got[own_rows, :] = v_send[seq]
 
     @pl.when(unit == 0)
     def _():
+        do_got[0, :, unit_rows, :] = do_send[seq]
         delta[0, unit_piece] = delta_send[pl.ds(pl.multiple_of(seq * 8, 8), 8), :]
-
-    @pl.when(unit != 0)
-    def _():
-        delta_copy(0).start()
 
     def from_everyone(copies):
         for k in range(1, seqs):
@@ -258,16 +282,18 @@
         def spread(x):
             return jnp.concatenate([jnp.where(mask, x, zero), jnp.where(mask, pltpu.roll(x, HEAD_WIDTH, 1), zero)], axis=0)
 
-        k_rows[at, :] = spread(raw).astype(BF16)
         scaled = raw * BASE2_SCALE
         high = scaled.astype(BF16).astype(F32)
-        rest = scaled - high
         within = pl.ds(pl.multiple_of(lax.rem(t, 2) * TILE, TILE), TILE)
         ks[within, 0:128] = spread(high).astype(BF16)
-        ks[within, 128:256] = spread(rest).astype(BF16)
+        ks[within, 128:256] = spread(scaled - high).astype(BF16)
         nothing = jnp.zeros((HEAD_WIDTH, TILE), F32)
-        ks_t[0:128, at] = jnp.concatenate([halves(high.T), nothing], axis=0).astype(BF16)
-        ks_t[128:256, at] = jnp.concatenate([halves(rest.T), aux_s], axis=0).astype(BF16)
+        turned = halves(raw.T)
+        k_rows[at, :] = spread(raw).astype(BF16)
+        scaled = turned * BASE2_SCALE
+        high = scaled.astype(BF16).astype(F32)
+        ks_t[0:128, at] = jnp.concatenate([high, nothing], axis=0).astype(BF16)
+        ks_t[128:256, at] = jnp.concatenate([scaled - high, aux_s], axis=0).astype(BF16)
 
     def prepare_values(t):
         at = pl.ds(pl.multiple_of(t * TILE, TILE), TILE)
@@ -282,56 +308,102 @@
 
     def stats(u, t, masked):
         w = ks[pl.ds(pl.multiple_of(lax.rem(t, 2) * TILE, TILE), TILE), :]
-        for h in range(QUERY_PER_KEY):
+        news = []
+
+        def scores(h):
             cols = pl.ds(h * TILE, TILE)
             s = dot(w, lt[u, :, cols], ((1,), (0,)))
             if masked:
                 s = jnp.where(place(0) <= place(1), s, NEG_LARGE)
-            old = stat_m[u, 0:1, cols]
-            new = jnp.maximum(old, jnp.max(s, axis=0, keepdims=True))
-            e = jnp.exp2(s - new)
-            part = jnp.sum(e.reshape(TILE // 8, 8, TILE), axis=0)
-            stat_l[u, :, cols] = stat_l[u, :, cols] * jnp.exp2(old - new) + part
-            stat_m[u, :, cols] = jnp.broadcast_to(new, (8, TILE))
-
-    def visit(block, step):
+            top = jnp.full((8, TILE), NEG_LARGE, F32)
+            for r in range(0, TILE, STRIP):
+                strip = s[r : r + STRIP]
+                s_buf[h, r : r + STRIP, :] = strip
+                for i in range(0, STRIP, 8):
+                    top = jnp.maximum(top, strip[i : i + 8])
+            news.append(jnp.maximum(stat_m[u, 0:1, cols], jnp.max(top, axis=0, keepdims=True)))
+
+        def sums(h):
+            cols = pl.ds(h * TILE, TILE)
+            new = jnp.broadcast_to(news[h], (8, TILE))
+            total = stat_l[u, :, cols] * jnp.exp2(stat_m[u, :, cols] - new)
+            for r in range(0, TILE, 8):
+                total = total + jnp.exp2(s_buf[h, r : r + 8, :] - new)
+            stat_l[u, :, cols] = total
+            stat_m[u, :, cols] = new
+
+        scores(0)
+        for h in range(1, QUERY_PER_KEY):
+            scores(h)
+            sums(h - 1)
+        sums(QUERY_PER_KEY - 1)
+
+    def visit(block, step, both=True, only=0):
         @pl.loop(0, 4)
         def _(i):
             u = lax.rem(i, 2)
             t = block * 2 + lax.div(i, 2)
             last = jnp.where(u == 0, 2 * own, key_tiles - 1 - 2 * own)
-
-            @pl.when(t < last)
+            wanted = jnp.logical_or(both, u == only)
+
+            @pl.when(jnp.logical_and(wanted, t < last))
             def _():
                 step(u, t, False)
 
-            @pl.when(t == last)
+            @pl.when(jnp.logical_and(wanted, t == last))
             def _():
                 step(u, t, True)
 
+    def arrives(k):
+        return jnp.logical_and(k > 0, jnp.logical_and(k < 11, k != 7))
+
     def cast_wait(k, got, send, receive):
-        at = pl.ds(pl.multiple_of(shifted(k, -1) * (block_len // 2), block_len // 2), block_len // 2)
-        remote(got.at[at], got.at[at], send.at[k], receive.at[k], shifted(k, 1), seq).wait_recv()
+        at = block_rows(shifted(k, -1))
+        remote(got.at[at], got.at[at], send.at[k], receive.at[k], place_before(k), seq).wait_recv()
 
     @pl.loop(0, spans)
-    def _(k):
+    def _(step):
+        k = lax.rem(spans - step, spans)
         block = shifted(k, -1)
 
+        for at_step, on in KEYS_ON:
+            @pl.when(step == at_step)
+            def _():
+                cast_wait(on, k_got, kcast_ss, kcast_rs)
+                pass_on(on, k_cast)
+
+        @pl.when(arrives(k))
+        def _():
+            cast_wait(k, k_got, kcast_ss, kcast_rs)
+
         @pl.when(needs(own, block))
         def _():
-            @pl.when(k > 0)
-            def _():
-                cast_wait(k, k_got, kcast_ss, kcast_rs)
-
             prepare_keys(2 * block)
             prepare_keys(2 * block + 1)
             visit(block, stats)
 
-            @pl.when(k == 0)
-            def _():
+        @pl.when(k == 0)
+        def _():
+            for copy in (v_copy, do_copy, delta_copy):
                 for i in range(1, seqs):
-                    v_copy(i).wait_recv()
-                cast_all(v_cast)
+                    copy(i).start()
+
+            @pl.when(unit != 0)
+            def _():
+                do_copy(0).start()
+                delta_copy(0).start()
+
+        @pl.when(step == VALUES_AT)
+        def _():
+            for i in range(1, seqs):
+                v_copy(i).wait_recv()
+            cast_all(v_cast)
+
+        for at_step, on in VALUES_ON:
+            @pl.when(step == at_step)
+            def _():
+                cast_wait(on, v_got, vcast_ss, vcast_rs)
+                pass_on(on, v_cast)
 
     from_everyone(delta_copy)
     from_everyone(do_copy)
@@ -355,96 +427,116 @@
             l2[u, h] = lt[u, 128:256, cols].astype(F32).T.astype(BF16)
 
     def main(u, t, masked):
+        slot = jnp.where(lax.div(t, 2) == own, 1, 0)
         at = pl.ds(pl.multiple_of(t * TILE, TILE), TILE)
         within = pl.ds(pl.multiple_of(lax.rem(t, 2) * TILE, TILE), TILE)
         kw = ks_t[:, at]
         vw = vs_t[:, at]
-        raw = k_rows[at, :]
+        kr = k_rows[at, :]
+
+        def products(h):
+            lhs = jnp.concatenate([l1[u, h], l2[u, h]], axis=1)
+            return dot(lhs, kw, ((1,), (0,))), dot(lhs, vw, ((1,), (0,)))
+
+        def weights(h, s, dp):
+            for r in range(0, TILE, STRIP):
+                here = pl.ds(h * TILE + r, STRIP)
+                p = jnp.exp2(s[r : r + STRIP])
+                if masked:
+                    p = jnp.where(place(1)[r : r + STRIP] <= place(0)[r : r + STRIP], p, 0.0)
+                p_buf[here, :] = p.astype(BF16)
+                ds_buf[here, :] = (p * dp[r : r + STRIP]).astype(BF16)
+
         for h in range(QUERY_PER_KEY):
+            weights(h, *products(h))
             here = pl.ds(h * TILE, TILE)
-            lhs = jnp.concatenate([l1[u, h], l2[u, h]], axis=1)
-            s = dot(lhs, kw, ((1,), (0,)))
-            dp = dot(lhs, vw, ((1,), (0,)))
-            p = jnp.exp2(s)
-            if masked:
-                p = jnp.where(place(1) <= place(0), p, 0.0)
-            ds = (p * dp).astype(BF16)
-            p_buf[here, :] = p.astype(BF16)
-            ds_buf[here, :] = ds
-            dq_acc[u, here, :] += dot(ds, raw, ((1,), (0,)))
-        dkv_acc[0:64, within] += dot(lt[u, 0:64, :], ds_buf[...], ((1,), (0,)))
-        dkv_acc[64:128, within] += dot(lt[u, 64:128, :], p_buf[...], ((1,), (0,)))
+            dq_acc[u, here, :] += dot(ds_buf[here, :], kr, ((1,), (0,)))
+        dkv_acc[slot, 0:64, within] += dot(lt[u, 0:64, :], ds_buf[...], ((1,), (0,)))
+        dkv_acc[slot, 64:128, within] += dot(lt[u, 64:128, :], p_buf[...], ((1,), (0,)))
 
     def part_copy(k):
         return remote(part_send.at[k], part_recv.at[k], part_ss.at[k], part_rs.at[k], shifted(k, -1), seq)
 
-    @pl.loop(1, spans + 1)
+    def dq_copy(j):
+        u, i = j // half, j % half
+        at_span = own if u == 0 else mirror
+        at = pl.ds(i * packed, packed)
+        return remote(dq_send.at[u, :, at, :], dq_recv.at[seq], dq_ss.at[j], dq_rs.at[seq], at_span, j)
+
+    def dq_arrival(g):
+        return remote(dq_send.at[0, :, pl.ds(0, packed), :], dq_recv.at[g], dq_ss.at[0], dq_rs.at[g], own, g)
+
+    def dq_pack(u):
+        mask = lax.broadcasted_iota(jnp.int32, (HALF, LANES), 1) < HEAD_WIDTH
+        for h in range(QUERY_PER_KEY):
+            first = dq_acc[u, h * TILE : h * TILE + HALF, :]
+            second = dq_acc[u, h * TILE + HALF : (h + 1) * TILE, :]
+            dq_send[u, h] = (jnp.where(mask, first, pltpu.roll(second, HEAD_WIDTH, 1)) * SCORE_SCALE).astype(BF16)
+
+    last_second = 0 * own
+    for k in range(1, spans):
+        last_second = jnp.where(shifted(k, -1) <= mirror, k, last_second)
+    dkv_acc[1] = jnp.zeros((LANES, block_len), F32)
+
+    @pl.loop(0, spans + 1)
     def _(j):
         k = lax.rem(j, spans)
         block = shifted(k, -1)
 
+        @pl.when(arrives(k))
+        def _():
+            cast_wait(k, v_got, vcast_ss, vcast_rs)
+
         @pl.when(needs(own, block))
         def _():
             @pl.when(k > 0)
             def _():
-                cast_wait(k, v_got, vcast_ss, vcast_rs)
-
-            prepare_values(2 * block)
-            prepare_values(2 * block + 1)
-            dkv_acc[...] = jnp.zeros((LANES, block_len), F32)
-            visit(block, main)
-            dkv_acc[0:64, :] = dkv_acc[0:64, :] * SCORE_SCALE
+                dkv_acc[0] = jnp.zeros((LANES, block_len), F32)
+
+            @pl.when(j < spans)
+            def _():
+                prepare_values(2 * block)
+                prepare_values(2 * block + 1)
+
+            visit(block, main, k > 0, jnp.where(j == 0, 1, 0))
 
             @pl.when(k > 0)
             def _():
-                part_send[k] = dkv_acc[...].astype(BF16)
+                part_send[k, 0:64, :] = (dkv_acc[0, 0:64, :] * SCORE_SCALE).astype(BF16)
+                part_send[k, 64:128, :] = dkv_acc[0, 64:128, :].astype(BF16)
                 part_copy(k).start()
 
-    even = lax.rem(seq, 2) == 0
-
-    def dq_copy(j):
-        u, i = j // half, j % half
-        at_span = own if u == 0 else mirror
-        return remote(dq_send.at[j], dq_recv.at[seq], dq_ss.at[j], dq_rs.at[seq], at_span, j)
-
-    def dq_arrival(g):
-        return remote(dq_send.at[0], dq_recv.at[g], dq_ss.at[0], dq_rs.at[g], own, g)
-
-    for j in range(seqs):
-        u, i = j // half, j % half
-        h0, h1, h2 = (
-            jnp.concatenate([dq_acc[u, at : at + packed, :], dq_acc[u, at + HALF : at + HALF + packed, :]], axis=0) * SCORE_SCALE
-            for at in (h * TILE + i * packed for h in range(QUERY_PER_KEY))
-        )
-        middle = pltpu.roll(h1, HEAD_WIDTH, 1)
-        first = jnp.where(even, jnp.where(low, h0, middle), pltpu.roll(h0, HEAD_WIDTH, 1))
-        second = jnp.where(even, h2, jnp.where(low, h1, pltpu.roll(h2, HEAD_WIDTH, 1)))
-        dq_send[j, 0] = first.astype(BF16)
-        dq_send[j, 1] = second.astype(BF16)
-        if u == 0:
-            @pl.when(seq == j)
-            def _():
-                dq_recv[j] = dq_send[j]
-
-            @pl.when(seq != j)
-            def _():
-                dq_copy(j).start()
-        else:
+        @pl.when(j == last_second)
+        def _():
+            dq_pack(1)
+            for i in range(half, seqs):
+                dq_copy(i).start()
+
+    dq_pack(0)
+    for j in range(half):
+        @pl.when(seq == j)
+        def _():
+            dq_recv[j] = dq_send[0, :, j * packed : (j + 1) * packed, :]
+
+        @pl.when(seq != j)
+        def _():
             dq_copy(j).start()
+
+    dkv_acc[1, 0:64, :] = dkv_acc[1, 0:64, :] * SCORE_SCALE
 
     @pl.loop(1, spans)
     def _(k):
         @pl.when(needs(shifted(k, 1), own))
         def _():
             part_copy(k).wait_recv()
-            dkv_acc[...] += part_recv[k].astype(F32)
+            dkv_acc[1] += part_recv[k].astype(F32)
 
     def grad_copy(k):
         there = seq_shifted(k, 1)
         return remote(grad_send.at[there], grad_recv.at[k], grad_ss.at[k], grad_rs.at[k], own, there)
 
     for j in range(seqs // half):
-        turned = dkv_acc[:, j * TILE : (j + 1) * TILE].T
+        turned = dkv_acc[1, :, j * TILE : (j + 1) * TILE].T
         for i in range(half):
             at = i * packed
             piece = jnp.concatenate([turned[at : at + packed], turned[at + HALF : at + HALF + packed]], axis=0)
@@ -460,12 +552,10 @@
         def _():
             dq_arrival(g).wait_recv()
 
-    for i in range(seqs // 2):
-        at = 3 * LANES * i
-        qg_out[0, :, at : at + LANES] = dq_recv[2 * i, 0]
-        both = jnp.where(low, dq_recv[2 * i, 1].astype(F32), dq_recv[2 * i + 1, 0].astype(F32))
-        qg_out[0, :, at + LANES : at + 2 * LANES] = both.astype(BF16)
-        qg_out[0, :, at + 2 * LANES : at + 3 * LANES] = dq_recv[2 * i + 1, 1]
+    for i in range(heads // 2):
+        a, b = (dq_recv[n // QUERY_PER_KEY, n % QUERY_PER_KEY].astype(F32) for n in (2 * i, 2 * i + 1))
+        at = slice(i * LANES, (i + 1) * LANES)
+        qg_out[0, :packed, at], qg_out[0, packed:, at] = paired(a, b)
 
     for k in range(1, seqs):
         grad_copy(k).wait_recv()
@@ -495,10 +585,8 @@
 
     @pl.loop(1, spans)
     def _(k):
-        @pl.when(needs(shifted(k, 1), own))
-        def _():
-            k_cast(k).wait_send()
-            v_cast(k).wait_send()
+        k_cast(k).wait_send()
+        v_cast(k).wait_send()
 
         @pl.when(needs(own, shifted(k, -1)))
         def _():
@@ -538,12 +626,13 @@
                 pltpu.VMEM((256, total), BF16),
                 pltpu.VMEM((256, total), BF16),
                 pltpu.VMEM((2 * TILE, 256), BF16),
+                pltpu.VMEM((QUERY_PER_KEY, TILE, TILE), F32),
                 pltpu.VMEM((2, 8, rows), F32),
                 pltpu.VMEM((2, 8, rows), F32),
                 pltpu.VMEM((2, rows, LANES), F32),
                 pltpu.VMEM((rows, TILE), BF16),
                 pltpu.VMEM((rows, TILE), BF16),
-                pltpu.VMEM((LANES, block_len), F32),
+                pltpu.VMEM((2, LANES, block_len), F32),
                 pltpu.VMEM((seqs, tokens // 2, LANES), BF16),
                 pltpu.VMEM((seqs, tokens // 2, LANES), BF16),
                 pltpu.VMEM((seqs, QUERY_PER_KEY, tokens // 2, LANES), BF16),
@@ -551,8 +640,8 @@
                 pltpu.VMEM((8 * seqs, tokens), F32),
                 pltpu.VMEM((spans, LANES, block_len), BF16),
                 pltpu.VMEM((spans, LANES, block_len), BF16),
-                pltpu.VMEM((seqs, 2, tokens, LANES), BF16),
-                pltpu.VMEM((seqs, 2, tokens, LANES), BF16),
+                pltpu.VMEM((2, QUERY_PER_KEY, HALF, LANES), BF16),
+                pltpu.VMEM((seqs, QUERY_PER_KEY, tokens // 2, LANES), BF16),
                 pltpu.VMEM((seqs, tokens, LANES), BF16),
                 pltpu.VMEM((seqs, tokens, LANES), BF16),
             ]

time: 164 us -> 166 us (1.012); the launches traced: 162 us -> 166 us
  Pallas kernels: 158 us -> 162 us
    pallas_call x1, Pallas kernels: 158 us -> 162 us  [per_device(): pl.pallas_call(functools.partial(fused_kernel, seqs, spans), out_shape=(j...]
where the time goes in v4:
time: 166 us
  Pallas kernels  162 us (98%)
  local copies, waits for them, and re-layouts  3.41 us (2%)
    pallas_call x1, Pallas kernels, per_device(): pl.pallas_call(functools.partial(fused_kernel, seqs, spans), out_shape=(j...  162 us
    unnamed x7, local copies, waits for them, and re-layouts  3.41 us

profile of v4, /device:TPU:99, one launch (start us, length us, event | category | flops | bytes accessed | tf_op | source)
XLA Modules:
  0.0 166.1 jit_solution(7803450940140308668)
XLA Ops:
  0.6 162.1 %attention_grads.1 = (bf16[1,128,1536]{2,1,0:T(8,128)(2,1)}, bf16[1,128,512]{2,1,0:T(8,128)(2,1)}, bf16[1,128,512]{2,1,0:T(8,128)(2,1)}) custom-call(bf16[1,128,1536]{2,1,0:T(8,128)(2,1)} %q_in.1, bf16[1,128,512]{2,1,0:T(8,128)(2,1)} %k_in.1, bf16[1,128,512]{2,1,0:T(8,128)(2,1)} %v_in.1, bf16[1,128,1536]{2,1,0:T(8,128)(2,1)} %o_in.1, bf16[1,128,1536]{2,1,0:T(8,128)(2,1)} %do_in.1), custom_call_target="tpu_custom_call" | custom-call | tf_op jit(solution)/shard_map/attention_grads/pallas_call | solution.py:607
  162.7 0.0 copy-start.1
  162.7 1.8 %copy.11 = bf16[1,128,1536]{2,1,0:T(8,128)(2,1)} copy(bf16[1,128,1536]{2,1,0:T(8,128)(2,1)} %get-tuple-element.6) | data formatting | bytes 786432
  164.5 0.0 copy-done.1
  164.5 0.0 copy-start
  164.5 0.7 copy.12
  165.2 0.3 copy-done
  165.5 0.7 copy.13
Async XLA Ops:
  162.7 1.8 %copy-start.1 = (bf16[1,128,512]{2,1,0:T(8,128)(2,1)S(1)}, bf16[1,128,512]{2,1,0:T(8,128)(2,1)}, u32[]{:S(2)}) copy-start(bf16[1,128,512]{2,1,0:T(8,128)(2,1)} %get-tuple-element.7) | copy-start | bytes 393220
  164.5 1.0 copy-start

commit v5 on v3

--- a/solution.py
+++ b/solution.py
@@ -12,6 +12,8 @@
 QUERY_PER_KEY = 3
 TILE = 512
 HALF = TILE // 2
+VALUES_AT = 6
+STRIP = 64
 LANES = 128
 NEG_LARGE = -1e30
 SCORE_SCALE = 1.0 / math.sqrt(HEAD_WIDTH)
@@ -32,7 +34,7 @@
 
 
 def fused_kernel(seqs, spans, q_in, k_in, v_in, o_in, do_in, qg_out, kg_out, vg_out, k_got, v_got, q_got, do_got, delta, lt, l1, l2, k_rows,
-                 ks_t, vs_t, ks, stat_m, stat_l, dq_acc, p_buf, ds_buf, dkv_acc, k_send, v_send, q_send, do_send, delta_send,
+                 ks_t, vs_t, ks, s_buf, stat_m, stat_l, dq_acc, p_buf, ds_buf, dkv_acc, k_send, v_send, q_send, do_send, delta_send,
                  part_send, part_recv, dq_send, dq_recv, grad_send, grad_recv, k_ss, k_rs, v_ss, v_rs, q_ss, q_rs, do_ss, do_rs,
                  delta_ss, delta_rs, kcast_ss, kcast_rs, vcast_ss, vcast_rs, part_ss, part_rs, dq_ss, dq_rs, grad_ss, grad_rs):
     own = lax.axis_index("span")
@@ -85,9 +87,6 @@
         def _():
             greet(there, seq)
 
-    lane = lax.broadcasted_iota(jnp.int32, (tokens, LANES), 1)
-    low = lane < HEAD_WIDTH
-
     def paired(a, b):
         mask = lax.broadcasted_iota(jnp.int32, a.shape, 1) < HEAD_WIDTH
         return (
@@ -179,20 +178,7 @@
     cast_all(k_cast)
 
     pack_keys(v_in, v_send)
-    for k in range(1, seqs):
-        v_copy(k).start()
-    v_got[own_rows, :] = v_send[seq]
     pack_queries(do_in, do_send)
-    for k in range(1, seqs):
-        do_copy(k).start()
-
-    @pl.when(unit == 0)
-    def _():
-        do_got[0, :, unit_rows, :] = do_send[seq]
-
-    @pl.when(unit != 0)
-    def _():
-        do_copy(0).start()
 
     head_row = lax.broadcasted_iota(jnp.int32, (8 * seqs, heads * HEAD_WIDTH), 0)
     head_col = lax.broadcasted_iota(jnp.int32, (8 * seqs, heads * HEAD_WIDTH), 1)
@@ -204,16 +190,12 @@
     product_high = product.astype(BF16)
     product_low = (product - product_high.astype(F32)).astype(BF16)
     delta_send[...] = dot(selector, product_high, ((1,), (1,))) + dot(selector, product_low, ((1,), (1,)))
-    for k in range(1, seqs):
-        delta_copy(k).start()
+    v_got[own_rows, :] = v_send[seq]
 
     @pl.when(unit == 0)
     def _():
+        do_got[0, :, unit_rows, :] = do_send[seq]
         delta[0, unit_piece] = delta_send[pl.ds(pl.multiple_of(seq * 8, 8), 8), :]
-
-    @pl.when(unit != 0)
-    def _():
-        delta_copy(0).start()
 
     def from_everyone(copies):
         for k in range(1, seqs):
@@ -258,16 +240,18 @@
         def spread(x):
             return jnp.concatenate([jnp.where(mask, x, zero), jnp.where(mask, pltpu.roll(x, HEAD_WIDTH, 1), zero)], axis=0)
 
-        k_rows[at, :] = spread(raw).astype(BF16)
         scaled = raw * BASE2_SCALE
         high = scaled.astype(BF16).astype(F32)
-        rest = scaled - high
         within = pl.ds(pl.multiple_of(lax.rem(t, 2) * TILE, TILE), TILE)
         ks[within, 0:128] = spread(high).astype(BF16)
-        ks[within, 128:256] = spread(rest).astype(BF16)
+        ks[within, 128:256] = spread(scaled - high).astype(BF16)
         nothing = jnp.zeros((HEAD_WIDTH, TILE), F32)
-        ks_t[0:128, at] = jnp.concatenate([halves(high.T), nothing], axis=0).astype(BF16)
-        ks_t[128:256, at] = jnp.concatenate([halves(rest.T), aux_s], axis=0).astype(BF16)
+        turned = halves(raw.T)
+        k_rows[at, :] = spread(raw).astype(BF16)
+        scaled = turned * BASE2_SCALE
+        high = scaled.astype(BF16).astype(F32)
+        ks_t[0:128, at] = jnp.concatenate([high, nothing], axis=0).astype(BF16)
+        ks_t[128:256, at] = jnp.concatenate([scaled - high, aux_s], axis=0).astype(BF16)
 
     def prepare_values(t):
         at = pl.ds(pl.multiple_of(t * TILE, TILE), TILE)
@@ -282,17 +266,35 @@
 
     def stats(u, t, masked):
         w = ks[pl.ds(pl.multiple_of(lax.rem(t, 2) * TILE, TILE), TILE), :]
-        for h in range(QUERY_PER_KEY):
+        news = []
+
+        def scores(h):
             cols = pl.ds(h * TILE, TILE)
             s = dot(w, lt[u, :, cols], ((1,), (0,)))
             if masked:
                 s = jnp.where(place(0) <= place(1), s, NEG_LARGE)
-            old = stat_m[u, 0:1, cols]
-            new = jnp.maximum(old, jnp.max(s, axis=0, keepdims=True))
-            e = jnp.exp2(s - new)
-            part = jnp.sum(e.reshape(TILE // 8, 8, TILE), axis=0)
-            stat_l[u, :, cols] = stat_l[u, :, cols] * jnp.exp2(old - new) + part
-            stat_m[u, :, cols] = jnp.broadcast_to(new, (8, TILE))
+            top = jnp.full((8, TILE), NEG_LARGE, F32)
+            for r in range(0, TILE, STRIP):
+                strip = s[r : r + STRIP]
+                s_buf[h, r : r + STRIP, :] = strip
+                for i in range(0, STRIP, 8):
+                    top = jnp.maximum(top, strip[i : i + 8])
+            news.append(jnp.maximum(stat_m[u, 0:1, cols], jnp.max(top, axis=0, keepdims=True)))
+
+        def sums(h):
+            cols = pl.ds(h * TILE, TILE)
+            new = jnp.broadcast_to(news[h], (8, TILE))
+            total = stat_l[u, :, cols] * jnp.exp2(stat_m[u, :, cols] - new)
+            for r in range(0, TILE, 8):
+                total = total + jnp.exp2(s_buf[h, r : r + 8, :] - new)
+            stat_l[u, :, cols] = total
+            stat_m[u, :, cols] = new
+
+        scores(0)
+        for h in range(1, QUERY_PER_KEY):
+            scores(h)
+            sums(h - 1)
+        sums(QUERY_PER_KEY - 1)
 
     def visit(block, step):
         @pl.loop(0, 4)
@@ -327,11 +329,22 @@
             prepare_keys(2 * block + 1)
             visit(block, stats)
 
-            @pl.when(k == 0)
-            def _():
+        @pl.when(k == 0)
+        def _():
+            for copy in (v_copy, do_copy, delta_copy):
                 for i in range(1, seqs):
-                    v_copy(i).wait_recv()
-                cast_all(v_cast)
+                    copy(i).start()
+
+            @pl.when(unit != 0)
+            def _():
+                do_copy(0).start()
+                delta_copy(0).start()
+
+        @pl.when(k == VALUES_AT)
+        def _():
+            for i in range(1, seqs):
+                v_copy(i).wait_recv()
+            cast_all(v_cast)
 
     from_everyone(delta_copy)
     from_everyone(do_copy)
@@ -359,19 +372,25 @@
         within = pl.ds(pl.multiple_of(lax.rem(t, 2) * TILE, TILE), TILE)
         kw = ks_t[:, at]
         vw = vs_t[:, at]
-        raw = k_rows[at, :]
+        kr = k_rows[at, :]
+
+        def products(h):
+            lhs = jnp.concatenate([l1[u, h], l2[u, h]], axis=1)
+            return dot(lhs, kw, ((1,), (0,))), dot(lhs, vw, ((1,), (0,)))
+
+        def weights(h, s, dp):
+            for r in range(0, TILE, STRIP):
+                here = pl.ds(h * TILE + r, STRIP)
+                p = jnp.exp2(s[r : r + STRIP])
+                if masked:
+                    p = jnp.where(place(1)[r : r + STRIP] <= place(0)[r : r + STRIP], p, 0.0)
+                p_buf[here, :] = p.astype(BF16)
+                ds_buf[here, :] = (p * dp[r : r + STRIP]).astype(BF16)
+
         for h in range(QUERY_PER_KEY):
+            weights(h, *products(h))
             here = pl.ds(h * TILE, TILE)
-            lhs = jnp.concatenate([l1[u, h], l2[u, h]], axis=1)
-            s = dot(lhs, kw, ((1,), (0,)))
-            dp = dot(lhs, vw, ((1,), (0,)))
-            p = jnp.exp2(s)
-            if masked:
-                p = jnp.where(place(1) <= place(0), p, 0.0)
-            ds = (p * dp).astype(BF16)
-            p_buf[here, :] = p.astype(BF16)
-            ds_buf[here, :] = ds
-            dq_acc[u, here, :] += dot(ds, raw, ((1,), (0,)))
+            dq_acc[u, here, :] += dot(ds_buf[here, :], kr, ((1,), (0,)))
         dkv_acc[0:64, within] += dot(lt[u, 0:64, :], ds_buf[...], ((1,), (0,)))
         dkv_acc[64:128, within] += dot(lt[u, 64:128, :], p_buf[...], ((1,), (0,)))
 
@@ -400,37 +419,33 @@
                 part_send[k] = dkv_acc[...].astype(BF16)
                 part_copy(k).start()
 
-    even = lax.rem(seq, 2) == 0
-
     def dq_copy(j):
         u, i = j // half, j % half
         at_span = own if u == 0 else mirror
-        return remote(dq_send.at[j], dq_recv.at[seq], dq_ss.at[j], dq_rs.at[seq], at_span, j)
+        at = pl.ds(i * packed, packed)
+        return remote(dq_send.at[u, :, at, :], dq_recv.at[seq], dq_ss.at[j], dq_rs.at[seq], at_span, j)
 
     def dq_arrival(g):
-        return remote(dq_send.at[0], dq_recv.at[g], dq_ss.at[0], dq_rs.at[g], own, g)
-
-    for j in range(seqs):
-        u, i = j // half, j % half
-        h0, h1, h2 = (
-            jnp.concatenate([dq_acc[u, at : at + packed, :], dq_acc[u, at + HALF : at + HALF + packed, :]], axis=0) * SCORE_SCALE
-            for at in (h * TILE + i * packed for h in range(QUERY_PER_KEY))
-        )
-        middle = pltpu.roll(h1, HEAD_WIDTH, 1)
-        first = jnp.where(even, jnp.where(low, h0, middle), pltpu.roll(h0, HEAD_WIDTH, 1))
-        second = jnp.where(even, h2, jnp.where(low, h1, pltpu.roll(h2, HEAD_WIDTH, 1)))
-        dq_send[j, 0] = first.astype(BF16)
-        dq_send[j, 1] = second.astype(BF16)
-        if u == 0:
-            @pl.when(seq == j)
-            def _():
-                dq_recv[j] = dq_send[j]
-
-            @pl.when(seq != j)
-            def _():
+        return remote(dq_send.at[0, :, pl.ds(0, packed), :], dq_recv.at[g], dq_ss.at[0], dq_rs.at[g], own, g)
+
+    for u in (1, 0):
+        for h in range(QUERY_PER_KEY):
+            mask = lax.broadcasted_iota(jnp.int32, (HALF, LANES), 1) < HEAD_WIDTH
+            first = dq_acc[u, h * TILE : h * TILE + HALF, :]
+            second = dq_acc[u, h * TILE + HALF : (h + 1) * TILE, :]
+            dq_send[u, h] = (jnp.where(mask, first, pltpu.roll(second, HEAD_WIDTH, 1)) * SCORE_SCALE).astype(BF16)
+        for i in range(half):
+            j = u * half + i
+            if u == 0:
+                @pl.when(seq == j)
+                def _():
+                    dq_recv[j] = dq_send[0, :, i * packed : (i + 1) * packed, :]
+
+                @pl.when(seq != j)
+                def _():
+                    dq_copy(j).start()
+            else:
                 dq_copy(j).start()
-        else:
-            dq_copy(j).start()
 
     @pl.loop(1, spans)
     def _(k):
@@ -460,12 +475,10 @@
         def _():
             dq_arrival(g).wait_recv()
 
-    for i in range(seqs // 2):
-        at = 3 * LANES * i
-        qg_out[0, :, at : at + LANES] = dq_recv[2 * i, 0]
-        both = jnp.where(low, dq_recv[2 * i, 1].astype(F32), dq_recv[2 * i + 1, 0].astype(F32))
-        qg_out[0, :, at + LANES : at + 2 * LANES] = both.astype(BF16)
-        qg_out[0, :, at + 2 * LANES : at + 3 * LANES] = dq_recv[2 * i + 1, 1]
+    for i in range(heads // 2):
+        a, b = (dq_recv[n // QUERY_PER_KEY, n % QUERY_PER_KEY].astype(F32) for n in (2 * i, 2 * i + 1))
+        at = slice(i * LANES, (i + 1) * LANES)
+        qg_out[0, :packed, at], qg_out[0, packed:, at] = paired(a, b)
 
     for k in range(1, seqs):
         grad_copy(k).wait_recv()
@@ -538,6 +551,7 @@
                 pltpu.VMEM((256, total), BF16),
                 pltpu.VMEM((256, total), BF16),
                 pltpu.VMEM((2 * TILE, 256), BF16),
+                pltpu.VMEM((QUERY_PER_KEY, TILE, TILE), F32),
                 pltpu.VMEM((2, 8, rows), F32),
                 pltpu.VMEM((2, 8, rows), F32),
                 pltpu.VMEM((2, rows, LANES), F32),
@@ -551,8 +565,8 @@
                 pltpu.VMEM((8 * seqs, tokens), F32),
                 pltpu.VMEM((spans, LANES, block_len), BF16),
                 pltpu.VMEM((spans, LANES, block_len), BF16),
-                pltpu.VMEM((seqs, 2, tokens, LANES), BF16),
-                pltpu.VMEM((seqs, 2, tokens, LANES), BF16),
+                pltpu.VMEM((2, QUERY_PER_KEY, HALF, LANES), BF16),
+                pltpu.VMEM((seqs, QUERY_PER_KEY, tokens // 2, LANES), BF16),
                 pltpu.VMEM((seqs, tokens, LANES), BF16),
                 pltpu.VMEM((seqs, tokens, LANES), BF16),
             ]

time: 164 us -> 158 us (0.963); the launches traced: 162 us -> 157 us
  Pallas kernels: 158 us -> 153 us
    pallas_call x1, Pallas kernels: 158 us -> 153 us  [per_device(): pl.pallas_call(functools.partial(fused_kernel, seqs, spans), out_shape=(j...]
where the time goes in v5:
time: 158 us; the launch traced here: 157 us
  Pallas kernels  153 us (97%)
  local copies, waits for them, and re-layouts  3.41 us (2%)
    pallas_call x1, Pallas kernels, per_device(): pl.pallas_call(functools.partial(fused_kernel, seqs, spans), out_shape=(j...  153 us
    unnamed x7, local copies, waits for them, and re-layouts  3.41 us

profile of v5, /device:TPU:99, one launch (start us, length us, event | category | flops | bytes accessed | tf_op | source)
XLA Modules:
  0.0 157.5 jit_solution(3741866620662349851)
XLA Ops:
  0.6 153.4 %attention_grads.1 = (bf16[1,128,1536]{2,1,0:T(8,128)(2,1)}, bf16[1,128,512]{2,1,0:T(8,128)(2,1)}, bf16[1,128,512]{2,1,0:T(8,128)(2,1)}) custom-call(bf16[1,128,1536]{2,1,0:T(8,128)(2,1)} %q_in.1, bf16[1,128,512]{2,1,0:T(8,128)(2,1)} %k_in.1, bf16[1,128,512]{2,1,0:T(8,128)(2,1)} %v_in.1, bf16[1,128,1536]{2,1,0:T(8,128)(2,1)} %o_in.1, bf16[1,128,1536]{2,1,0:T(8,128)(2,1)} %do_in.1), custom_call_target="tpu_custom_call" | custom-call | tf_op jit(solution)/shard_map/attention_grads/pallas_call | solution.py:532
  154.0 0.0 copy-start.1
  154.0 1.8 %copy.11 = bf16[1,128,1536]{2,1,0:T(8,128)(2,1)} copy(bf16[1,128,1536]{2,1,0:T(8,128)(2,1)} %get-tuple-element.6) | data formatting | bytes 786432
  155.8 0.0 copy-done.1
  155.8 0.0 copy-start
  155.8 0.7 copy.12
  156.5 0.3 copy-done
  156.8 0.7 copy.13
Async XLA Ops:
  154.0 1.8 %copy-start.1 = (bf16[1,128,512]{2,1,0:T(8,128)(2,1)S(1)}, bf16[1,128,512]{2,1,0:T(8,128)(2,1)}, u32[]{:S(2)}) copy-start(bf16[1,128,512]{2,1,0:T(8,128)(2,1)} %get-tuple-element.7) | copy-start | bytes 393220
  155.8 1.0 copy-start

commit v6 on v5

--- a/solution.py
+++ b/solution.py
@@ -397,6 +397,27 @@
     def part_copy(k):
         return remote(part_send.at[k], part_recv.at[k], part_ss.at[k], part_rs.at[k], shifted(k, -1), seq)
 
+    def dq_copy(j):
+        u, i = j // half, j % half
+        at_span = own if u == 0 else mirror
+        at = pl.ds(i * packed, packed)
+        return remote(dq_send.at[u, :, at, :], dq_recv.at[seq], dq_ss.at[j], dq_rs.at[seq], at_span, j)
+
+    def dq_arrival(g):
+        return remote(dq_send.at[0, :, pl.ds(0, packed), :], dq_recv.at[g], dq_ss.at[0], dq_rs.at[g], own, g)
+
+    def dq_pack(u):
+        mask = lax.broadcasted_iota(jnp.int32, (HALF, LANES), 1) < HEAD_WIDTH
+        for h in range(QUERY_PER_KEY):
+            first = dq_acc[u, h * TILE : h * TILE + HALF, :]
+            second = dq_acc[u, h * TILE + HALF : (h + 1) * TILE, :]
+            dq_send[u, h] = (jnp.where(mask, first, pltpu.roll(second, HEAD_WIDTH, 1)) * SCORE_SCALE).astype(BF16)
+
+    last_second = 0 * own
+    for k in range(1, spans):
+        last_second = jnp.where(shifted(k, -1) <= mirror, k, last_second)
+    last_second = jnp.where(own <= mirror, spans, last_second)
+
     @pl.loop(1, spans + 1)
     def _(j):
         k = lax.rem(j, spans)
@@ -419,33 +440,21 @@
                 part_send[k] = dkv_acc[...].astype(BF16)
                 part_copy(k).start()
 
-    def dq_copy(j):
-        u, i = j // half, j % half
-        at_span = own if u == 0 else mirror
-        at = pl.ds(i * packed, packed)
-        return remote(dq_send.at[u, :, at, :], dq_recv.at[seq], dq_ss.at[j], dq_rs.at[seq], at_span, j)
-
-    def dq_arrival(g):
-        return remote(dq_send.at[0, :, pl.ds(0, packed), :], dq_recv.at[g], dq_ss.at[0], dq_rs.at[g], own, g)
-
-    for u in (1, 0):
-        for h in range(QUERY_PER_KEY):
-            mask = lax.broadcasted_iota(jnp.int32, (HALF, LANES), 1) < HEAD_WIDTH
-            first = dq_acc[u, h * TILE : h * TILE + HALF, :]
-            second = dq_acc[u, h * TILE + HALF : (h + 1) * TILE, :]
-            dq_send[u, h] = (jnp.where(mask, first, pltpu.roll(second, HEAD_WIDTH, 1)) * SCORE_SCALE).astype(BF16)
-        for i in range(half):
-            j = u * half + i
-            if u == 0:
-                @pl.when(seq == j)
-                def _():
-                    dq_recv[j] = dq_send[0, :, i * packed : (i + 1) * packed, :]
-
-                @pl.when(seq != j)
-                def _():
-                    dq_copy(j).start()
-            else:
-                dq_copy(j).start()
+        @pl.when(j == last_second)
+        def _():
+            dq_pack(1)
+            for i in range(half, seqs):
+                dq_copy(i).start()
+
+    dq_pack(0)
+    for j in range(half):
+        @pl.when(seq == j)
+        def _():
+            dq_recv[j] = dq_send[0, :, j * packed : (j + 1) * packed, :]
+
+        @pl.when(seq != j)
+        def _():
+            dq_copy(j).start()
 
     @pl.loop(1, spans)
     def _(k):

time: 158 us -> 158 us (level)
  no operation moved by 1% of the time
where the time goes in v6:
time: 158 us
  Pallas kernels  154 us (97%)
  local copies, waits for them, and re-layouts  3.41 us (2%)
    pallas_call x1, Pallas kernels, per_device(): pl.pallas_call(functools.partial(fused_kernel, seqs, spans), out_shape=(j...  154 us
    unnamed x7, local copies, waits for them, and re-layouts  3.41 us

profile of v6, /device:TPU:99, one launch (start us, length us, event | category | flops | bytes accessed | tf_op | source)
XLA Modules:
  0.0 158.3 jit_solution(14459575436280097781)
XLA Ops:
  0.6 154.2 %attention_grads.1 = (bf16[1,128,1536]{2,1,0:T(8,128)(2,1)}, bf16[1,128,512]{2,1,0:T(8,128)(2,1)}, bf16[1,128,512]{2,1,0:T(8,128)(2,1)}) custom-call(bf16[1,128,1536]{2,1,0:T(8,128)(2,1)} %q_in.1, bf16[1,128,512]{2,1,0:T(8,128)(2,1)} %k_in.1, bf16[1,128,512]{2,1,0:T(8,128)(2,1)} %v_in.1, bf16[1,128,1536]{2,1,0:T(8,128)(2,1)} %o_in.1, bf16[1,128,1536]{2,1,0:T(8,128)(2,1)} %do_in.1), custom_call_target="tpu_custom_call" | custom-call | tf_op jit(solution)/shard_map/attention_grads/pallas_call | solution.py:541
  154.9 0.0 copy-start.1
  154.9 1.8 %copy.11 = bf16[1,128,1536]{2,1,0:T(8,128)(2,1)} copy(bf16[1,128,1536]{2,1,0:T(8,128)(2,1)} %get-tuple-element.6) | data formatting | bytes 786432
  156.7 0.0 copy-done.1
  156.7 0.0 copy-start
  156.7 0.7 copy.12
  157.3 0.3 copy-done
  157.6 0.7 copy.13
Async XLA Ops:
  154.9 1.8 %copy-start.1 = (bf16[1,128,512]{2,1,0:T(8,128)(2,1)S(1)}, bf16[1,128,512]{2,1,0:T(8,128)(2,1)}, u32[]{:S(2)}) copy-start(bf16[1,128,512]{2,1,0:T(8,128)(2,1)} %get-tuple-element.7) | copy-start | bytes 393220
  156.7 1.0 copy-start
